TPU v7x, 256 devices: a whole 4x4x8 slice. The times are simulated.
256 devices in a mesh: pass: 64 (over x, z, y_hi), cell: 4 (over y_lo, core).
Axes of the slice: x: 4, y: 4 (y_hi: 2, y_lo: 2; y = y_hi * 2 + y_lo), z: 8, core: 2. Of those that a mesh axis runs over, the one named last changes fastest.
Arguments:
- flow_state: float32 [16384, 4096], P('pass', 'cell'), may hold values from -6 to 6
- face_weights: float32 [4, 16384, 4096], P(None, 'pass', 'cell'), may hold values from 0.02 to 0.24
- forcing: float32 [16384, 4096], P('pass', 'cell'), may hold values from -1.2 to 1.2
- lagged_planes: float32 [64, 8, 4096], P('pass', None, 'cell'), may hold values from -6 to 6
- phase_lag: int32 [32, 2], replicated, may hold values from 0 to 8
- face_map: int32 [64, 4096], P('pass', 'cell'), may hold values from 0 to 4095, as said below
- surface_record: bfloat16 [64, 120, 4096], P('pass', None, 'cell'), may hold values from -6 to 6
- face_radius: float32 [2, 4096], P(None, 'cell'), may hold values from 0.3 to 1
- face_angle: float32 [2, 4096], P(None, 'cell'), may hold values from -0.3 to 0.3
- face_axial: float32 [2, 4096], P(None, 'cell'), may hold values from -0.3 to 0.3
- face_stagger: float32 [2, 4096], P(None, 'cell'), may hold values from -1.2 to 1.2
- face_area: float32 [2, 4096], P(None, 'cell'), may hold values from 0.5 to 1.5
- listeners: float32 [3, 1024], replicated, as said below
- observer_group: int32 [1024], replicated, may hold values from 0 to 15
Outputs:
- final_field: float32 [16384, 4096], P('pass', 'cell')
- acoustic: float32 [1024, 128], P('cell')
- array_signal: float32 [16, 128], replicated
Inputs may be any that keep to these rules, and one draw needn't show every extreme that they name: face_map[j, a] lies in the aligned block of 1024 axial indices that holds a, and for each j the entries of a block are a permutation of that block. `listeners`: every observer is between 1.3 and 4 from the anchor.
All inputs are finite; a program needn't handle non-finite values.
Results may differ from a plain program's by a relative error of at most 0.0035.
Values sent between devices are 32-bit elements; how exact they have to be, the bound alone decides.
No kernel may reach another device: no remote copies, remote signals or barrier semaphores. Data moves between devices by JAX's collectives and lax.ppermute only.
A program may use at most 64 MiB of HBM per device.

v0:
```python
import functools
import math

import jax
import jax.numpy as jnp
from jax import lax
from jax.experimental import pallas as pl
from jax.experimental.pallas import tpu as pltpu
from jax.sharding import Mesh
from jax.sharding import PartitionSpec as P

STEPS = 8
GROUPS = 16
sound_speed = 2.0

W = 1024
E = 128
WX = W + E
TOP = 16 + 256
ROWS = TOP + 16
SPLIT = {"x": 4, "z": 8, "y_hi": 2}
PASS = ("x", "z", "y_hi")
VMEM_LIMIT = 24 * 1024 * 1024
F32 = jnp.float32


def params(**kw):
    return pltpu.CompilerParams(vmem_limit_bytes=VMEM_LIMIT, **kw)


def vmem():
    return pl.BlockSpec(memory_space=pltpu.VMEM)


def smem():
    return pl.BlockSpec(memory_space=pltpu.SMEM)


def place():
    index = lax.axis_index("x") * (SPLIT["z"] * SPLIT["y_hi"]) + lax.axis_index("z") * SPLIT["y_hi"]
    index = index + lax.axis_index("y_hi")
    return index // 2, index % 2


def strips_body(field, weights, forcing, lagged, maps, to_mid, to_plane, sems):
    _, half = place()
    mid = pl.multiple_of(jnp.where(half == 0, 248, 0), 8)
    plane = pl.multiple_of(jnp.where(half == 0, 0, 248), 8)
    copies = []
    for out, start in ((to_mid, mid), (to_plane, plane)):
        rows = pl.ds(start, 8)
        copies.append((field.at[rows], out.at[pl.ds(0, 8)]))
        for i in range(4):
            copies.append((weights.at[i, rows], out.at[pl.ds(8 + 8 * i, 8)]))
        copies.append((forcing.at[rows], out.at[pl.ds(40, 8)]))
    copies.append((lagged.at[0], to_plane.at[pl.ds(48, 8)]))
    started = []
    for n, (source, target) in enumerate(copies):
        copy = pltpu.make_async_copy(source, target, sems.at[n])
        copy.start()
        started.append(copy)
    to_plane[56:64, :] = jnp.broadcast_to(maps[...].astype(F32), (8, W))
    for copy in started:
        copy.wait()


def strips(field, weights, forcing, lagged, maps):
    anywhere = pl.BlockSpec(memory_space=pl.ANY)
    return pl.pallas_call(
        strips_body,
        out_shape=(jax.ShapeDtypeStruct((48, W), F32), jax.ShapeDtypeStruct((64, W), F32)),
        in_specs=[anywhere, anywhere, anywhere, anywhere, vmem()],
        out_specs=(vmem(), vmem()),
        scratch_shapes=[pltpu.SemaphoreType.DMA((13,))],
        compiler_params=params(),
        name="strips",
    )(field, weights, forcing, lagged, maps)


def square(row):
    tiles = [row[:, 128 * s : 128 * (s + 1)] for s in range(8)]
    return jnp.concatenate(tiles, axis=0).astype(jnp.int32) & (W - 1)


def level_row(level):
    return jnp.where(level >= 0, 8 + level, -level - 1)


def picked(history, level, index):
    row = level_row(level)
    high, low = index >> 7, index & 127
    tiles = history[row]
    out = jnp.zeros((8, 128), F32)
    for b in range(8):
        source = jnp.broadcast_to(tiles[b : b + 1, :], (8, 128))
        value = jnp.take_along_axis(source, low, axis=1, mode="promise_in_bounds")
        out = jnp.where(high == b, value, out)
    return out


def keep_row(history, row, array, at):
    for b in range(8):
        history[row, b : b + 1, :] = array[at : at + 1, 128 * b : 128 * (b + 1)]


def keep_lagged(history, lagged):
    for j in range(8):
        for b in range(8):
            history[j, b : b + 1, :] = lagged[j : j + 1, 128 * b : 128 * (b + 1)]


def put_row(array, row, value):
    for s in range(8):
        array[row : row + 1, 128 * s : 128 * (s + 1)] = value[s : s + 1, :]


def fill_gaps(array, own, other, index, lags, half, level):
    main = pl.ds(0, W)

    @pl.when(half == 0)
    def _():
        keep_row(own, 8 + level, array, 16)
        keep_row(other, 8 + level, array, 7)

    @pl.when(half == 1)
    def _():
        keep_row(own, 8 + level, array, TOP - 1)
        keep_row(other, 8 + level, array, TOP + 8)

    mine = picked(other, level - lags[0], index[0])
    theirs = picked(own, level - lags[1], index[1])

    @pl.when(half == 0)
    def _():
        put_row(array, 15, mine)
        put_row(array, 8, theirs)
        array[TOP : TOP + 1, main] = array[TOP + 8 : TOP + 9, main]
        array[TOP + 7 : TOP + 8, main] = array[TOP - 1 : TOP, main]

    @pl.when(half == 1)
    def _():
        put_row(array, TOP, mine)
        put_row(array, TOP + 7, theirs)
        array[15:16, main] = array[7:8, main]
        array[8:9, main] = array[16:17, main]


def lag_pair(phase_lag, passage, half):
    count = phase_lag.shape[0]
    beside = lax.rem(passage + 2 * half - 1 + count, count)
    return phase_lag[passage, half], phase_lag[beside, 1 - half]


def relaxed(current, before, after, weights, forcing, width):
    sub = lax.broadcasted_iota(jnp.int32, (8, width), 0)
    inner = current[:, :width]
    below = jnp.where(sub == 0, pltpu.roll(before[:, :width], 1, 0), pltpu.roll(inner, 1, 0))
    above = jnp.where(sub == 7, pltpu.roll(after[:, :width], 7, 0), pltpu.roll(inner, 7, 0))
    left = pltpu.roll(current, 1, 1)[:, :width]
    right = pltpu.roll(current, WX - 1, 1)[:, :width]
    low = weights[0] * (below - inner) + weights[1] * (above - inner)
    side = weights[2] * (left - inner) + weights[3] * (right - inner)
    return (inner + forcing) + (low + side)


def step(source, target, weights, forcing, strip, rim, width, strips_too):
    def joined(own, edge):
        return own if width == W else jnp.concatenate([own, edge], axis=1)

    def one(start, row):
        own = pl.ds(row, 8)
        at = pl.ds(start, 8)
        w = [joined(weights[i, own, :], rim[i, at, :]) for i in range(4)]
        f = joined(forcing[own, :], rim[4, at, :])
        new = relaxed(
            source[at, :], source[pl.ds(start - 8, 8), :], source[pl.ds(start + 8, 8), :], w, f, width
        )
        return new

    def tile(t, carry):
        row = pl.multiple_of(8 * t, 8)
        start = pl.multiple_of(16 + 8 * t, 8)
        new = one(start, row)
        if target.shape[0] == ROWS:
            target[pl.ds(start, 8), :width] = new
        else:
            target[pl.ds(row, 8), :width] = new
        return carry

    lax.fori_loop(0, 32, tile, 0, unroll=2)
    if strips_too:
        for start, first, before, after in ((0, 0, 0, 8), (ROWS - 8, 8, ROWS - 16, ROWS - 8)):
            at = slice(start, start + 8)
            w = [joined(strip[i, first : first + 8, :], rim[i, at, :]) for i in range(4)]
            f = joined(strip[4, first : first + 8, :], rim[4, at, :])
            target[at, :width] = relaxed(
                source[at, :], source[before : before + 8, :], source[after : after + 8, :], w, f, width
            )


def strip_tiles(from_mid, from_plane, half, row, lanes):
    mid = from_mid[row : row + 8, lanes]
    plane = from_plane[row : row + 8, lanes]
    return jnp.where(half == 0, plane, mid), jnp.where(half == 0, mid, plane)


def edges_body(
    first, last, u_l, u_r, w_l, w_r, f_l, f_r, lagged, maps, from_mid, from_plane, phase_lag, to_left, to_right,
    array, own, other,
):
    passage, half = place()
    full = slice(0, W)
    bottom, top = strip_tiles(from_mid, from_plane, half, 0, full)
    array[0:8, :] = bottom
    array[ROWS - 8 : ROWS, :] = top
    array[16:24, :] = first[...]
    array[TOP - 8 : TOP, :] = last[...]
    array[8:16, :] = jnp.zeros((8, W), F32)
    array[TOP : TOP + 8, :] = jnp.zeros((8, W), F32)
    keep_lagged(own, lagged.at[0])
    keep_lagged(other, from_plane.at[48:56])
    index = (square(maps[...]), square(from_plane[56:57, :]))
    fill_gaps(array, own, other, index, lag_pair(phase_lag, passage, half), half, 0)

    for out, block, u, w, f, sign in ((to_left, 0, u_l, w_l, f_l, 1), (to_right, 7, u_r, w_r, f_r, -1)):
        lanes = slice(128 * block, 128 * (block + 1))

        def packed(value, extra):
            lane = lax.broadcasted_iota(jnp.int32, value.shape, 1)
            for i, e in enumerate(extra):
                spot = 2 + i if sign == 1 else 125 - i
                value = jnp.where(lane == spot, pltpu.roll(e, (sign * (2 + i)) % 128, 1), value)
            return value

        out[16:TOP, :] = packed(u[...], [w[0], w[1], w[2], w[3], f[...]])
        pairs = [strip_tiles(from_mid, from_plane, half, 8 * i, lanes) for i in range(6)]
        out[0:8, :] = packed(pairs[0][0], [p[0] for p in pairs[1:]])
        out[ROWS - 8 : ROWS, :] = packed(pairs[0][1], [p[1] for p in pairs[1:]])
        out[8:16, :] = array[8:16, lanes]
        out[TOP : TOP + 8, :] = array[TOP : TOP + 8, lanes]


def edges(field, weights, forcing, lagged, maps, from_mid, from_plane, phase_lag):
    def spec(shape, *at):
        return pl.BlockSpec(shape, lambda i: at)

    whole = [spec((1, 8, W), 0, 0, 0), spec((1, W), 0, 0), spec((48, W), 0, 0), spec((64, W), 0, 0), smem()]
    return pl.pallas_call(
        edges_body,
        grid=(1,),
        out_shape=(jax.ShapeDtypeStruct((ROWS, E), F32),) * 2,
        in_specs=[
            spec((8, W), 0, 0),
            spec((8, W), 31, 0),
            spec((256, E), 0, 0),
            spec((256, E), 0, 7),
            spec((4, 256, E), 0, 0, 0),
            spec((4, 256, E), 0, 0, 7),
            spec((256, E), 0, 0),
            spec((256, E), 0, 7),
            *whole,
        ],
        out_specs=(spec((ROWS, E), 0, 0),) * 2,
        scratch_shapes=[pltpu.VMEM((ROWS, W), F32), pltpu.VMEM((16, 8, 128), F32), pltpu.VMEM((16, 8, 128), F32)],
        compiler_params=params(),
        name="edges",
    )(field, field, field, field, weights, weights, forcing, forcing, lagged, maps, from_mid, from_plane, phase_lag)


def set_rim(array, from_left, from_right):
    lane = lax.broadcasted_iota(jnp.int32, (ROWS, E), 1)
    array[:, W:] = jnp.where(lane < 64, from_right[...], from_left[...])


def finish(level, source, between, out, surface, weights, forcing, strip, rim, own, other, index, lags, half, tail):
    step(source, between, weights, forcing, strip, rim, WX, True)
    surface[0:1, :] = between[16 + 128 : 17 + 128, :W]
    fill_gaps(between, own, other, index, lags, half, level + 1)
    step(between, out, weights, forcing, strip, rim, W, not tail)
    row = 128 if tail else 16 + 128
    surface[1:2, :] = out[row : row + 1, :]
    surface[2:8, :] = jnp.zeros((6, W), F32)


def first_body(
    field, weights, forcing, lagged, maps, from_mid, from_plane, from_left, from_right, phase_lag,
    out, to_left, to_right, surface, own, other, strip, rim, index, source, between,
):
    passage, half = place()
    full = slice(0, W)
    bottom, top = strip_tiles(from_mid, from_plane, half, 0, full)
    source[0:8, :W] = bottom
    source[ROWS - 8 : ROWS, :W] = top
    source[16:TOP, :W] = field[...]
    source[8:16, :W] = jnp.zeros((8, W), F32)
    source[TOP : TOP + 8, :W] = jnp.zeros((8, W), F32)
    set_rim(source, from_left, from_right)
    lane = lax.broadcasted_iota(jnp.int32, (ROWS, E), 1)
    for i in range(5):
        bottom, top = strip_tiles(from_mid, from_plane, half, 8 + 8 * i, full)
        strip[i, 0:8, :] = bottom
        strip[i, 8:16, :] = top
        right = pltpu.roll(from_right[...], 128 - (2 + i), 1)
        left = pltpu.roll(from_left[...], 2 + i, 1)
        rim[i, :, :] = jnp.where(lane == 0, right, jnp.where(lane == 127, left, 0.0))
    keep_lagged(own, lagged.at[0])
    keep_lagged(other, from_plane.at[48:56])
    own[8:16] = jnp.zeros((8, 8, 128), F32)
    other[8:16] = jnp.zeros((8, 8, 128), F32)
    index[0:8, :] = square(maps[...])
    index[8:16, :] = square(from_plane[56:57, :])
    pair = (index[0:8, :], index[8:16, :])
    lags = lag_pair(phase_lag, passage, half)
    fill_gaps(source, own, other, pair, lags, half, 0)
    out[8:16, :] = jnp.zeros((8, W), F32)
    out[TOP : TOP + 8, :] = jnp.zeros((8, W), F32)
    between[8:16, :] = jnp.zeros((8, WX), F32)
    between[TOP : TOP + 8, :] = jnp.zeros((8, WX), F32)
    finish(0, source, between, out, surface, weights, forcing, strip, rim, own, other, pair, lags, half, False)
    fill_gaps(out, own, other, pair, lags, half, 2)
    to_left[...] = out[:, :E]
    to_right[...] = out[:, W - E :]


def next_body(
    level, tail, state, weights, forcing, from_left, from_right, own_in, other_in, strip, rim, index, phase_lag, *rest
):
    if tail:
        out, surface, own, other, source, between = rest
    else:
        out, to_left, to_right, surface, own, other, source, between = rest
    passage, half = place()
    own[...] = own_in[...]
    other[...] = other_in[...]
    source[:, :W] = state[...]
    set_rim(source, from_left, from_right)
    between[8:16, :] = jnp.zeros((8, WX), F32)
    between[TOP : TOP + 8, :] = jnp.zeros((8, WX), F32)
    pair = (index[0:8, :], index[8:16, :])
    lags = lag_pair(phase_lag, passage, half)
    finish(level, source, between, out, surface, weights, forcing, strip, rim, own, other, pair, lags, half, tail)
    if not tail:
        out[8:16, :] = jnp.zeros((8, W), F32)
        out[TOP : TOP + 8, :] = jnp.zeros((8, W), F32)
        fill_gaps(out, own, other, pair, lags, half, level + 2)
        to_left[...] = out[:, :E]
        to_right[...] = out[:, W - E :]


HISTORY = jax.ShapeDtypeStruct((16, 8, 128), F32)
EDGE = jax.ShapeDtypeStruct((ROWS, E), F32)
STATE = jax.ShapeDtypeStruct((ROWS, W), F32)
BUFFERS = [pltpu.VMEM((ROWS, WX), F32), pltpu.VMEM((ROWS, WX), F32)]
COST = pl.CostEstimate(flops=2 * 16 * 330 * 1024, bytes_accessed=8 << 20, transcendentals=0)


def first_steps(field, weights, forcing, lagged, maps, from_mid, from_plane, from_left, from_right, phase_lag):
    outs = (
        STATE, EDGE, EDGE, jax.ShapeDtypeStruct((8, W), F32), HISTORY, HISTORY,
        jax.ShapeDtypeStruct((5, 16, W), F32), jax.ShapeDtypeStruct((5, ROWS, E), F32),
        jax.ShapeDtypeStruct((16, 128), jnp.int32),
    )
    return pl.pallas_call(
        first_body,
        out_shape=outs,
        in_specs=[vmem()] * 9 + [smem()],
        out_specs=tuple(vmem() for _ in outs),
        scratch_shapes=BUFFERS,
        compiler_params=params(),
        cost_estimate=COST,
        name="steps_first",
    )(field, weights, forcing, lagged, maps, from_mid, from_plane, from_left, from_right, phase_lag)


def next_steps(level, state, weights, forcing, from_left, from_right, own, other, strip, rim, index, phase_lag):
    tail = level == STEPS - 2
    surface = jax.ShapeDtypeStruct((8, W), F32)
    if tail:
        outs = (jax.ShapeDtypeStruct((256, W), F32), surface)
        scratch = [pltpu.VMEM((16, 8, 128), F32), pltpu.VMEM((16, 8, 128), F32), *BUFFERS]
    else:
        outs = (STATE, EDGE, EDGE, surface, HISTORY, HISTORY)
        scratch = BUFFERS
    return pl.pallas_call(
        functools.partial(next_body, level, tail),
        out_shape=outs,
        in_specs=[vmem()] * 10 + [smem()],
        out_specs=tuple(vmem() for _ in outs),
        scratch_shapes=scratch,
        compiler_params=params(),
        cost_estimate=COST,
        name=f"steps_{level}",
    )(state, weights, forcing, from_left, from_right, own, other, strip, rim, index, phase_lag)


def kernels_body(points, radius, angle, axial, stagger, area, press, change, *, scale, passages):
    passage, half = place()

    def mine(ref):
        return jnp.where(half == 0, ref[0:1, :], ref[1:2, :])

    phase = passage.astype(F32) * (2.0 * math.pi / passages) + mine(angle)
    cos_phase, sin_phase = jnp.cos(phase), jnp.sin(phase)
    cos_stagger = jnp.cos(mine(stagger))
    weight = mine(area) * (scale / (4.0 * math.pi))
    normal_x = -weight * cos_stagger * sin_phase
    normal_y = weight * cos_stagger * cos_phase
    normal_z = weight * jnp.sin(mine(stagger))
    face_x = mine(radius) * cos_phase
    face_y = mine(radius) * sin_phase
    face_z = mine(axial)

    def tile(t, carry):
        rows = pl.ds(pl.multiple_of(16 * t, 16), 16)
        at = points[rows, :]
        delta_x = at[:, 0:1] - face_x
        delta_y = at[:, 1:2] - face_y
        delta_z = at[:, 2:3] - face_z
        inverse = lax.rsqrt(delta_x * delta_x + delta_y * delta_y + delta_z * delta_z)
        along = normal_x * delta_x + normal_y * delta_y + normal_z * delta_z
        both = along * inverse * inverse
        press[rows, :] = (both * inverse).astype(jnp.bfloat16)
        change[rows, :] = (both * (1.0 / sound_speed)).astype(jnp.bfloat16)
        return carry

    lax.fori_loop(0, press.shape[0] // 16, tile, 0)


def kernels(points, radius, angle, axial, stagger, area, part, count, scale, passages):
    size = points.shape[0] // count
    faces = pl.BlockSpec((2, W), lambda i: (0, 0))
    shape = jax.ShapeDtypeStruct((size, W), jnp.bfloat16)
    return pl.pallas_call(
        functools.partial(kernels_body, scale=scale, passages=passages),
        grid=(1,),
        out_shape=(shape, shape),
        in_specs=[pl.BlockSpec((size, 3), lambda i: (part, 0))] + [faces] * 5,
        out_specs=(pl.BlockSpec((size, W), lambda i: (0, 0)),) * 2,
        compiler_params=params(),
        cost_estimate=pl.CostEstimate(flops=20 * size * W, bytes_accessed=4 * size * W, transcendentals=size * W),
        name=f"kernels_{part}",
    )(points, radius, angle, axial, stagger, area)


def sound_body(*refs):
    presses, changes, (record, s0, s1, s2, s3, group, out, total) = refs[:4], refs[4:8], refs[8:]
    late = jnp.concatenate([s[0:2, :] for s in (s0, s1, s2, s3)], axis=0).astype(jnp.bfloat16)
    surface = jnp.concatenate([record[0].astype(F32), late.astype(F32)], axis=0)
    times = surface.shape[0]
    row = lax.broadcasted_iota(jnp.int32, surface.shape, 0)
    after, before = pltpu.roll(surface, times - 1, 0), pltpu.roll(surface, 1, 0)
    first = row == 0
    last = row == times - 1
    rate = jnp.where(last, surface, after) - jnp.where(first, surface, before)
    rate = jnp.where(first | last, rate, rate * 0.5).astype(jnp.bfloat16)
    surface = surface.astype(jnp.bfloat16)
    turned = (((1,), (1,)), ((), ()))
    size = presses[0].shape[0]
    for n in range(4):
        got = lax.dot_general(presses[n][...], surface, turned, preferred_element_type=F32)
        got = got + lax.dot_general(changes[n][...], rate, turned, preferred_element_type=F32)
        total[size * n : size * (n + 1), :] = got
    label = lax.broadcasted_iota(jnp.int32, (GROUPS, group.shape[1]), 0)
    member = (group[...] == label).astype(F32)
    counts = jnp.sum(member, axis=1, keepdims=True)
    means = jnp.dot(member, total[...], precision=lax.Precision.HIGHEST, preferred_element_type=F32)
    means = means / jnp.maximum(counts, 1.0)
    for s in range(8):
        for c in range(4):
            start = 256 * c + 32 * s
            out[4 * s + c, 0:32, :] = total[start : start + 32, :]
            out[4 * s + c, 32:34, :] = means[2 * s : 2 * s + 2, :]
            out[4 * s + c, 34:40, :] = jnp.zeros((6, 128), F32)


def sound(presses, changes, record, surfaces, group):
    return pl.pallas_call(
        sound_body,
        out_shape=jax.ShapeDtypeStruct((32, 40, 128), F32),
        in_specs=[vmem()] * 14,
        out_specs=vmem(),
        scratch_shapes=[pltpu.VMEM((1024, 128), F32)],
        compiler_params=params(),
        name="sound",
    )(*presses, *changes, record, *surfaces, group)


def exchanged(pieces, axes):
    return lax.all_to_all(pieces, axes, 0, 0, tiled=True)


def sent_to_all(block, axes):
    count = lax.axis_size(axes)
    return exchanged(jnp.broadcast_to(block, (count, *block.shape)), axes)


def on_device(
    flow_state,
    face_weights,
    forcing,
    lagged_planes,
    phase_lag,
    face_map,
    surface_record,
    face_radius,
    face_angle,
    face_axial,
    face_stagger,
    face_area,
    listeners,
    observer_group,
):
    passes = lax.axis_size(PASS)
    cells = lax.axis_size("cell")
    scale = 64.0 / math.sqrt(W * cells * passes)
    across = [(i, i ^ 1) for i in range(passes)]
    over = [(i, ((i + 1) ^ 1) - 1 if 0 < i < passes - 1 else passes - 1 - i) for i in range(passes)]
    rightward = [(i, i + 1) for i in range(cells - 1)]
    leftward = [(i + 1, i) for i in range(cells - 1)]

    to_mid, to_plane = strips(flow_state, face_weights, forcing, lagged_planes, face_map)
    from_mid = lax.ppermute(to_mid, PASS, across)
    from_plane = lax.ppermute(to_plane, PASS, over)

    points = listeners.T
    pairs = [
        kernels(points, face_radius, face_angle, face_axial, face_stagger, face_area, n, 4, scale, passes // 2)
        for n in range(4)
    ]

    to_left, to_right = edges(
        flow_state, face_weights, forcing, lagged_planes, face_map, from_mid, from_plane, phase_lag
    )
    from_left = lax.ppermute(to_right, "cell", rightward)
    from_right = lax.ppermute(to_left, "cell", leftward)
    state, to_left, to_right, surface, own, other, strip, rim, index = first_steps(
        flow_state, face_weights, forcing, lagged_planes, face_map, from_mid, from_plane, from_left, from_right,
        phase_lag,
    )
    surfaces = [surface]
    for level in range(2, STEPS, 2):
        from_left = lax.ppermute(to_right, "cell", rightward)
        from_right = lax.ppermute(to_left, "cell", leftward)
        got = next_steps(
            level, state, face_weights, forcing, from_left, from_right, own, other, strip, rim, index, phase_lag
        )
        if level < STEPS - 2:
            state, to_left, to_right, surface, own, other = got
        else:
            state, surface = got
        surfaces.append(surface)

    pieces = sound(
        [p[0] for p in pairs], [p[1] for p in pairs], surface_record, surfaces, observer_group[None, :]
    )
    part = jnp.sum(exchanged(pieces, ("x", "y_hi", "cell")), axis=0)
    part = jnp.sum(sent_to_all(part, "z"), axis=0)
    parts = sent_to_all(part, ("x", "y_hi"))
    acoustic = parts[:, :32].reshape(256, 128)
    array_signal = parts[:, 32:34].reshape(GROUPS, 128)
    return state, acoustic, array_signal


def solution(mesh):
    sizes = tuple(SPLIT.values())
    fine = Mesh(mesh.devices.reshape(*sizes, mesh.shape["cell"]), (*PASS, "cell"))
    return jax.shard_map(
        on_device,
        mesh=fine,
        in_specs=(
            P(PASS, "cell"),
            P(None, PASS, "cell"),
            P(PASS, "cell"),
            P(PASS, None, "cell"),
            P(),
            P(PASS, "cell"),
            P(PASS, None, "cell"),
            P(None, "cell"),
            P(None, "cell"),
            P(None, "cell"),
            P(None, "cell"),
            P(None, "cell"),
            P(),
            P(),
        ),
        out_specs=(P(PASS, "cell"), P("cell", None), P()),
        check_vma=False,
    )
```

profile of v0, /device:TPU:2, one launch (start us, length us, event | category | flops | bytes accessed | tf_op | source)
XLA Modules:
  0.0 146.6 jit_solution(18080910468747320864)
XLA Ops:
  0.6 2.2 %copy-done = f32[4,256,1024]{2,1,0:T(8,128)S(1)} copy-done((f32[4,256,1024]{2,1,0:T(8,128)S(1)}, f32[4,256,1024]{2,1,0:T(8,128)}, u32[]{:S(2)}) %copy-start) | copy-done | bytes 4194328
  2.8 1.2 copy-done.4
  4.0 1.2 copy-done.6
  5.3 0.8 copy-done.12
  6.0 0.7 copy-done.24
  6.7 0.7 strips.1
  7.5 8.5 %collective-permute-start.1 = (f32[64,1024]{1,0:T(8,128)S(1)}, f32[64,1024]{1,0:T(8,128)S(1)}, u32[]{:S(2)}, u32[]{:S(2)}) collective-permute-start(f32[64,1024]{1,0:T(8,128)S(1)} %get-tuple-element.39), channel_id=1, source_target_pairs={{0,252},{4,8},{8,4},{12,16},{16,12},{20,24},{24,20},{28,32},{32,28... | collective-permute-start | bytes 786440 | tf_op jit(solution)/shard_map/ppermute | solution.py:523
  16.0 0.1 copy.23.phase_lag
  16.1 10.4 %collective-permute-done.from_mid = f32[48,1024]{1,0:T(8,128)S(1)} collective-permute-done((f32[48,1024]{1,0:T(8,128)S(1)}, f32[48,1024]{1,0:T(8,128)S(1)}, u32[]{:S(2)}, u32[]{:S(2)}) %collective-permute-start) | collective-permute-done | bytes 196640 | tf_op jit(solution)/shard_map/ppermute | solution.py:522
  26.6 0.0 copy-start.1
  26.6 2.2 %copy-done.1 = f32[4,256,1024]{2,1,0:T(8,128)S(1)} copy-done((f32[4,256,1024]{2,1,0:T(8,128)S(1)}, f32[4,256,1024]{2,1,0:T(8,128)}, u32[]{:S(2)}) %copy-start.1) | copy-done | bytes 4194328
  28.8 1.5 %edges.1 = (f32[288,128]{1,0:T(8,128)S(1)}, f32[288,128]{1,0:T(8,128)S(1)}) custom-call(f32[256,1024]{1,0:T(8,128)S(1)} %copy-done.7, f32[256,1024]{1,0:T(8,128)S(1)} %copy-done.7, f32[256,1024]{1,0:T(8,128)S(1)} %copy-done.7, f32[256,1024]{1,0:T(8,128)S(1)} %copy-done.7, f32[4,256,1024]{2,1,0:T(8,128)S(1)} %copy-done.1, f32[4,256,1024]{2,1,0:T(8,128)S(1)} %copy-done.1, ...), custom_call_target="tpu_custom_call" | custom-call | tf_op jit(solution)/shard_map/edges/pallas_call | solution.py:248
  30.4 1.9 %collective-permute-start.2 = (f32[288,128]{1,0:T(8,128)S(1)}, f32[288,128]{1,0:T(8,128)S(1)}, u32[]{:S(2)}, u32[]{:S(2)}) collective-permute-start(f32[288,128]{1,0:T(8,128)S(1)} %get-tuple-element.40), channel_id=1, source_target_pairs={{0,1},{1,2},{2,3},{4,5},{5,6},{6,7},{8,9},{9,10},{10,11},{12,13},{... | collective-permute-start | bytes 442376 | tf_op jit(solution)/shard_map/ppermute | solution.py:534
  32.3 1.3 collective-permute-start.3
  33.6 2.2 %collective-permute-done.3.from_right = f32[288,128]{1,0:T(8,128)S(1)} collective-permute-done((f32[288,128]{1,0:T(8,128)S(1)}, f32[288,128]{1,0:T(8,128)S(1)}, u32[]{:S(2)}, u32[]{:S(2)}) %collective-permute-start.3) | collective-permute-done | bytes 147488 | tf_op jit(solution)/shard_map/ppermute | solution.py:535
  35.8 0.9 copy-done.11
  36.8 5.6 %steps_first.1 = (f32[288,1024]{1,0:T(8,128)S(1)}, f32[288,128]{1,0:T(8,128)S(1)}, f32[288,128]{1,0:T(8,128)S(1)}, f32[8,1024]{1,0:T(8,128)S(1)}, f32[16,8,128]{...) custom-call(f32[256,1024]{1,0:T(8,128)S(1)} %copy-done.7, ...), custom_call_target="tpu_custom_call" | custom-call | flops 10813440 | bytes 8388608 | tf_op jit(solution)/shard_map/steps_first/pallas_call | solution.py:363
  42.4 5.6 %collective-permute-start.4 = (f32[288,128]{1,0:T(8,128)S(1)}, f32[288,128]{1,0:T(8,128)S(1)}, u32[]{:S(2)}, u32[]{:S(2)}) collective-permute-start(f32[288,128]{1,0:T(8,128)S(1)} %get-tuple-element.43), channel_id=1, source_target_pairs={{0,1},{1,2},{2,3},{4,5},{5,6},{6,7},{8,9},{9,10},{10,11},{12,13},{... | collective-permute-start | bytes 442376 | tf_op jit(solution)/shard_map/ppermute | solution.py:542
  48.0 1.3 collective-permute-start.5
  49.3 2.0 %collective-permute-done.5.from_right = f32[288,128]{1,0:T(8,128)S(1)} collective-permute-done((f32[288,128]{1,0:T(8,128)S(1)}, f32[288,128]{1,0:T(8,128)S(1)}, u32[]{:S(2)}, u32[]{:S(2)}) %collective-permute-start.5) | collective-permute-done | bytes 147488 | tf_op jit(solution)/shard_map/ppermute | solution.py:543
  51.3 5.1 %steps_2.1 = (f32[288,1024]{1,0:T(8,128)S(1)}, f32[288,128]{1,0:T(8,128)S(1)}, f32[288,128]{1,0:T(8,128)S(1)}, f32[8,1024]{1,0:T(8,128)S(1)}, f32[16,8,128]{2,1,0:T(8,128)S(1)}, /*index=5*/f32[16,8,128]{2,1,0:T(8,128)S(1)}) custom-call(f32[288,1024]{1,0:T(8,128)S(1)} %get-tuple-element.42.state, f32[4,256,1024]{2,1,0:T(8,128)S(1)} %copy-done.2, ...), custom_call_target="tpu_custom_call" | custom-call | flops 10813440 | bytes 8388608 | tf_op jit(solution)/shard_map/steps_2/pallas_call | solution.py:384
  56.4 0.6 copy-done.28
  57.0 5.1 %collective-permute-start.6 = (f32[288,128]{1,0:T(8,128)S(1)}, f32[288,128]{1,0:T(8,128)S(1)}, u32[]{:S(2)}, u32[]{:S(2)}) collective-permute-start(f32[288,128]{1,0:T(8,128)S(1)} %get-tuple-element.51), channel_id=1, source_target_pairs={{0,1},{1,2},{2,3},{4,5},{5,6},{6,7},{8,9},{9,10},{10,11},{12,13},{... | collective-permute-start | bytes 442376 | tf_op jit(solution)/shard_map/ppermute | solution.py:542
  62.1 1.3 collective-permute-start.7
  63.4 2.0 %collective-permute-done.7.from_right = f32[288,128]{1,0:T(8,128)S(1)} collective-permute-done((f32[288,128]{1,0:T(8,128)S(1)}, f32[288,128]{1,0:T(8,128)S(1)}, u32[]{:S(2)}, u32[]{:S(2)}) %collective-permute-start.7) | collective-permute-done | bytes 147488 | tf_op jit(solution)/shard_map/ppermute | solution.py:543
  65.4 0.0 copy-start.21
  65.4 5.8 %steps_4.1 = (f32[288,1024]{1,0:T(8,128)S(1)}, f32[288,128]{1,0:T(8,128)}, f32[288,128]{1,0:T(8,128)}, f32[8,1024]{1,0:T(8,128)S(1)}, f32[16,8,128]{2,1,0:T(8,128)S(1)}, /*index=5*/f32[16,8,128]{2,1,0:T(8,128)S(1)}) custom-call(f32[288,1024]{1,0:T(8,128)S(1)} %get-tuple-element.50.state, f32[4,256,1024]{2,1,0:T(8,128)S(1)} %copy-done.2, ...), custom_call_target="tpu_custom_call" | custom-call | flops 10813440 | bytes 8388608 | tf_op jit(solution)/shard_map/steps_4/pallas_call | solution.py:384
  71.2 1.1 copy-done.8
  72.2 0.6 copy-done.30
  72.8 5.1 %collective-permute-start.8 = (f32[288,128]{1,0:T(8,128)}, f32[288,128]{1,0:T(8,128)S(1)}, u32[]{:S(2)}, u32[]{:S(2)}) collective-permute-start(f32[288,128]{1,0:T(8,128)} %get-tuple-element.56), channel_id=1, source_target_pairs={{0,1},{1,2},{2,3},{4,5},{5,6},{6,7},{8,9},{9,10},{10,11},{12,13},{... | collective-permute-start | bytes 442376 | tf_op jit(solution)/shard_map/ppermute | solution.py:542
  78.0 1.3 collective-permute-start.9
  79.3 0.2 copy.28
  79.5 2.0 %kernels_0.1 = (bf16[256,1024]{1,0:T(8,128)(2,1)S(1)}, bf16[256,1024]{1,0:T(8,128)(2,1)S(1)}) custom-call(f32[1024,3]{1,0:T(8,128)S(1)} %bitcast.4, f32[2,1024]{1,0:T(2,128)S(1)} %copy-done.17, f32[2,1024]{1,0:T(2,128)S(1)} %copy-done.18, f32[2,1024]{1,0:T(2,128)S(1)} %copy-done.19, f32[2,1024]{1,0:T(2,128)S(1)} %copy-done.20, f32[2,1024]{1,0:T(2,128)S(1)} %copy-done.21), custom_call_target="tpu_custom_call" | custom-call | flops 5242880 | bytes 1048576 | tf_op jit(solution)/shard_map/kernels_0/pallas_call | solution.py:433
  81.6 2.0 %kernels_1.1 = (bf16[256,1024]{1,0:T(8,128)(2,1)S(1)}, bf16[256,1024]{1,0:T(8,128)(2,1)S(1)}) custom-call(f32[1024,3]{1,0:T(8,128)S(1)} %bitcast.5, f32[2,1024]{1,0:T(2,128)S(1)} %copy-done.17, f32[2,1024]{1,0:T(2,128)S(1)} %copy-done.18, f32[2,1024]{1,0:T(2,128)S(1)} %copy-done.19, f32[2,1024]{1,0:T(2,128)S(1)} %copy-done.20, f32[2,1024]{1,0:T(2,128)S(1)} %copy-done.21), custom_call_target="tpu_custom_call" | custom-call | flops 5242880 | bytes 1048576 | tf_op jit(solution)/shard_map/kernels_1/pallas_call | solution.py:433
  83.6 2.0 %kernels_2.1 = (bf16[256,1024]{1,0:T(8,128)(2,1)S(1)}, bf16[256,1024]{1,0:T(8,128)(2,1)S(1)}) custom-call(f32[1024,3]{1,0:T(8,128)S(1)} %bitcast.6, f32[2,1024]{1,0:T(2,128)S(1)} %copy-done.17, f32[2,1024]{1,0:T(2,128)S(1)} %copy-done.18, f32[2,1024]{1,0:T(2,128)S(1)} %copy-done.19, f32[2,1024]{1,0:T(2,128)S(1)} %copy-done.20, f32[2,1024]{1,0:T(2,128)S(1)} %copy-done.21), custom_call_target="tpu_custom_call" | custom-call | flops 5242880 | bytes 1048576 | tf_op jit(solution)/shard_map/kernels_2/pallas_call | solution.py:433
  85.6 2.0 %kernels_3.1 = (bf16[256,1024]{1,0:T(8,128)(2,1)S(1)}, bf16[256,1024]{1,0:T(8,128)(2,1)S(1)}) custom-call(f32[1024,3]{1,0:T(8,128)S(1)} %bitcast.7, f32[2,1024]{1,0:T(2,128)S(1)} %copy-done.17, f32[2,1024]{1,0:T(2,128)S(1)} %copy-done.18, f32[2,1024]{1,0:T(2,128)S(1)} %copy-done.19, f32[2,1024]{1,0:T(2,128)S(1)} %copy-done.20, f32[2,1024]{1,0:T(2,128)S(1)} %copy-done.21), custom_call_target="tpu_custom_call" | custom-call | flops 5242880 | bytes 1048576 | tf_op jit(solution)/shard_map/kernels_3/pallas_call | solution.py:433
  87.6 0.7 copy-done.15
  88.3 2.2 %copy-done.3 = f32[4,256,1024]{2,1,0:T(8,128)S(1)} copy-done((f32[4,256,1024]{2,1,0:T(8,128)S(1)}, f32[4,256,1024]{2,1,0:T(8,128)}, u32[]{:S(2)}) %copy-start.3) | copy-done | bytes 4194328
  90.5 0.9 copy-done.16
  91.4 0.8 copy-done.23
  92.3 6.1 %steps_6.1 = (f32[256,1024]{1,0:T(8,128)}, f32[8,1024]{1,0:T(8,128)S(1)}) custom-call(f32[288,1024]{1,0:T(8,128)S(1)} %copy-done.9, f32[4,256,1024]{2,1,0:T(8,128)S(1)} %copy-done.3, f32[256,1024]{1,0:T(8,128)S(1)} %copy-done.5, f32[288,128]{1,0:T(8,128)S(1)} %copy-done.16, f32[288,128]{1,0:T(8,128)} %collective-permute-done.9.from_right, ...), custom_call_target="tpu_custom_call" | custom-call | flops 10813440 | bytes 8388608 | tf_op jit(solution)/shard_map/steps_6/pallas_call | solution.py:384
  98.3 1.5 %sound.1 = f32[32,40,128]{2,1,0:T(8,128)S(1)} custom-call(bf16[256,1024]{1,0:T(8,128)(2,1)S(1)} %get-tuple-element.61.refs_0_, bf16[256,1024]{1,0:T(8,128)(2,1)S(1)} %get-tuple-element.62.refs_1_, bf16[256,1024]{1,0:T(8,128)(2,1)S(1)} %get-tuple-element.63.refs_2_, bf16[256,1024]{1,0:T(8,128)(2,1)S(1)} %get-tuple-element.64.refs_3_, ...), custom_call_target="tpu_custom_call" | custom-call | tf_op jit(solution)/shard_map/sound/pallas_call | solution.py:477
  99.9 17.3 %all_to_all.15 = f32[32,40,128]{2,1,0:T(8,128)S(1)} all-to-all(f32[32,40,128]{2,1,0:T(8,128)S(1)} %sound.1), channel_id=1, replica_groups=mesh['x'=4,'z'=8,'y_hi'=2,'cell'=4] {'x','y_hi','cell'}, dimensions={0} | all-to-all | bytes 1310720 | tf_op jit(solution)/shard_map/all_to_all | solution.py:489
  117.2 0.1 reduce_sum.18
  117.2 17.2 %all_to_all.16 = f32[8,40,128]{2,1,0:T(8,128)S(1)} all-to-all(f32[8,40,128]{2,1,0:T(8,128)S(1)} %broadcast_in_dim.10), channel_id=1, replica_groups=mesh['x'=4,'z'=8,'y_hi'=2,'cell'=4] {'z'}, dimensions={0} | all-to-all | bytes 327680 | tf_op jit(solution)/shard_map/all_to_all | solution.py:489
  134.4 10.8 %all_to_all.17 = f32[8,40,128]{2,1,0:T(8,128)S(1)} all-to-all(f32[8,40,128]{2,1,0:T(8,128)S(1)} %broadcast_in_dim.11), channel_id=1, replica_groups=mesh['x'=4,'z'=8,'y_hi'=2,'cell'=4] {'x','y_hi'}, dimensions={0} | all-to-all | bytes 327680 | tf_op jit(solution)/shard_map/all_to_all | solution.py:489
  145.3 0.7 slice.8
  146.0 0.6 slice.9
  (64 shorter events, 0.2 us)
Async XLA Ops:
  0.6 2.2 %copy-start = (f32[4,256,1024]{2,1,0:T(8,128)S(1)}, f32[4,256,1024]{2,1,0:T(8,128)}, u32[]{:S(2)}) copy-start(f32[4,256,1024]{2,1,0:T(8,128)} %weights.9) | copy-start | bytes 12582916
  2.8 1.2 copy-start.4
  4.0 1.2 copy-start.6
  5.3 0.8 copy-start.12
  6.0 0.7 copy-start.24
  6.7 9.3 %copy-start.34 = (s32[32,2]{0,1:T(2,128)S(1)}, s32[32,2]{0,1:T(2,128)}, u32[]{:S(2)}) copy-start(s32[32,2]{0,1:T(2,128)} %param.18) | copy-start | bytes 772
  6.7 19.8 %copy-start.5 = (f32[256,1024]{1,0:T(8,128)S(1)}, f32[256,1024]{1,0:T(8,128)}, u32[]{:S(2)}) copy-start(f32[256,1024]{1,0:T(8,128)} %forcing.9) | copy-start | bytes 3145732
  6.7 19.8 %copy-start.7 = (f32[256,1024]{1,0:T(8,128)S(1)}, f32[256,1024]{1,0:T(8,128)}, u32[]{:S(2)}) copy-start(f32[256,1024]{1,0:T(8,128)} %field.3) | copy-start | bytes 3145732
  6.7 19.8 %copy-start.13 = (f32[1,8,1024]{2,1,0:T(8,128)S(1)}, f32[1,8,1024]{2,1,0:T(8,128)}, u32[]{:S(2)}) copy-start(f32[1,8,1024]{2,1,0:T(8,128)} %lagged.5) | copy-start | bytes 98308
  6.7 19.8 %copy-start.25 = (s32[1,1024]{1,0:T(1,128)S(1)}, s32[1,1024]{1,0:T(1,128)}, u32[]{:S(2)}) copy-start(s32[1,1024]{1,0:T(1,128)} %maps.5) | copy-start | bytes 12292
  7.5 19.1 %collective-permute-start.1 = (f32[64,1024]{1,0:T(8,128)S(1)}, f32[64,1024]{1,0:T(8,128)S(1)}, u32[]{:S(2)}, u32[]{:S(2)}) collective-permute-start(f32[64,1024]{1,0:T(8,128)S(1)} %get-tuple-element.39), channel_id=1, source_target_pairs={{0,252},{4,8},{8,4},{12,16},{16,12},{20,24},{24,20},{28,32},{32,28... | collective-permute-start | bytes 786440 | tf_op jit(solution)/shard_map/ppermute | solution.py:523
  16.0 10.5 %collective-permute-start = (f32[48,1024]{1,0:T(8,128)S(1)}, f32[48,1024]{1,0:T(8,128)S(1)}, u32[]{:S(2)}, u32[]{:S(2)}) collective-permute-start(f32[48,1024]{1,0:T(8,128)S(1)} %get-tuple-element.38), channel_id=1, source_target_pairs={{0,4},{4,0},{8,12},{12,8},{16,20},{20,16},{24,28},{28,24},{32,36},... | collective-permute-start | bytes 589832 | tf_op jit(solution)/shard_map/ppermute | solution.py:522
  26.5 3.8 %copy-start.10 = (f32[48,1024]{1,0:T(8,128)}, f32[48,1024]{1,0:T(8,128)S(1)}, u32[]{:S(2)}) copy-start(f32[48,1024]{1,0:T(8,128)S(1)} %collective-permute-done.from_mid) | copy-start | bytes 589828
  26.6 2.2 %copy-start.1 = (f32[4,256,1024]{2,1,0:T(8,128)S(1)}, f32[4,256,1024]{2,1,0:T(8,128)}, u32[]{:S(2)}) copy-start(f32[4,256,1024]{2,1,0:T(8,128)} %weights.9) | copy-start | bytes 12582916
  30.4 3.2 %collective-permute-start.2 = (f32[288,128]{1,0:T(8,128)S(1)}, f32[288,128]{1,0:T(8,128)S(1)}, u32[]{:S(2)}, u32[]{:S(2)}) collective-permute-start(f32[288,128]{1,0:T(8,128)S(1)} %get-tuple-element.40), channel_id=1, source_target_pairs={{0,1},{1,2},{2,3},{4,5},{5,6},{6,7},{8,9},{9,10},{10,11},{12,13},{... | collective-permute-start | bytes 442376 | tf_op jit(solution)/shard_map/ppermute | solution.py:534
  32.3 3.5 %collective-permute-start.3 = (f32[288,128]{1,0:T(8,128)S(1)}, f32[288,128]{1,0:T(8,128)S(1)}, u32[]{:S(2)}, u32[]{:S(2)}) collective-permute-start(f32[288,128]{1,0:T(8,128)S(1)} %get-tuple-element.41), channel_id=1, source_target_pairs={{1,0},{2,1},{3,2},{5,4},{6,5},{7,6},{9,8},{10,9},{11,10},{13,12},{... | collective-permute-start | bytes 442376 | tf_op jit(solution)/shard_map/ppermute | solution.py:535
  35.8 0.9 copy-start.11
  36.8 14.5 %copy-start.2 = (f32[4,256,1024]{2,1,0:T(8,128)S(1)}, f32[4,256,1024]{2,1,0:T(8,128)}, u32[]{:S(2)}) copy-start(f32[4,256,1024]{2,1,0:T(8,128)} %weights.9) | copy-start | bytes 12582916
  42.4 14.0 %copy-start.26 = (f32[8,1024]{1,0:T(8,128)}, f32[8,1024]{1,0:T(8,128)S(1)}, u32[]{:S(2)}) copy-start(f32[8,1024]{1,0:T(8,128)S(1)} %get-tuple-element.69.refs_9_) | copy-start | bytes 98308
  42.4 6.9 %collective-permute-start.4 = (f32[288,128]{1,0:T(8,128)S(1)}, f32[288,128]{1,0:T(8,128)S(1)}, u32[]{:S(2)}, u32[]{:S(2)}) collective-permute-start(f32[288,128]{1,0:T(8,128)S(1)} %get-tuple-element.43), channel_id=1, source_target_pairs={{0,1},{1,2},{2,3},{4,5},{5,6},{6,7},{8,9},{9,10},{10,11},{12,13},{... | collective-permute-start | bytes 442376 | tf_op jit(solution)/shard_map/ppermute | solution.py:542
  48.0 3.3 %collective-permute-start.5 = (f32[288,128]{1,0:T(8,128)S(1)}, f32[288,128]{1,0:T(8,128)S(1)}, u32[]{:S(2)}, u32[]{:S(2)}) collective-permute-start(f32[288,128]{1,0:T(8,128)S(1)} %get-tuple-element.44), channel_id=1, source_target_pairs={{1,0},{2,1},{3,2},{5,4},{6,5},{7,6},{9,8},{10,9},{11,10},{13,12},{... | collective-permute-start | bytes 442376 | tf_op jit(solution)/shard_map/ppermute | solution.py:543
  56.4 0.6 copy-start.28
  57.0 6.4 %collective-permute-start.6 = (f32[288,128]{1,0:T(8,128)S(1)}, f32[288,128]{1,0:T(8,128)S(1)}, u32[]{:S(2)}, u32[]{:S(2)}) collective-permute-start(f32[288,128]{1,0:T(8,128)S(1)} %get-tuple-element.51), channel_id=1, source_target_pairs={{0,1},{1,2},{2,3},{4,5},{5,6},{6,7},{8,9},{9,10},{10,11},{12,13},{... | collective-permute-start | bytes 442376 | tf_op jit(solution)/shard_map/ppermute | solution.py:542
  62.1 3.3 %collective-permute-start.7 = (f32[288,128]{1,0:T(8,128)S(1)}, f32[288,128]{1,0:T(8,128)S(1)}, u32[]{:S(2)}, u32[]{:S(2)}) collective-permute-start(f32[288,128]{1,0:T(8,128)S(1)} %get-tuple-element.52), channel_id=1, source_target_pairs={{1,0},{2,1},{3,2},{5,4},{6,5},{7,6},{9,8},{10,9},{11,10},{13,12},{... | collective-permute-start | bytes 442376 | tf_op jit(solution)/shard_map/ppermute | solution.py:543
  65.3 13.9 %copy-start.33 = (f32[3,1024]{1,0:T(4,128)S(1)}, f32[3,1024]{1,0:T(4,128)}, u32[]{:S(2)}) copy-start(f32[3,1024]{1,0:T(4,128)} %param.26) | copy-start | bytes 36868
  65.4 14.2 %copy-start.17 = (f32[2,1024]{1,0:T(2,128)S(1)}, f32[2,1024]{1,0:T(2,128)}, u32[]{:S(2)}) copy-start(f32[2,1024]{1,0:T(2,128)} %radius.7) | copy-start | bytes 24580
  65.4 14.2 %copy-start.18 = (f32[2,1024]{1,0:T(2,128)S(1)}, f32[2,1024]{1,0:T(2,128)}, u32[]{:S(2)}) copy-start(f32[2,1024]{1,0:T(2,128)} %angle.7) | copy-start | bytes 24580
  65.4 14.2 %copy-start.19 = (f32[2,1024]{1,0:T(2,128)S(1)}, f32[2,1024]{1,0:T(2,128)}, u32[]{:S(2)}) copy-start(f32[2,1024]{1,0:T(2,128)} %axial.7) | copy-start | bytes 24580
  65.4 14.2 %copy-start.20 = (f32[2,1024]{1,0:T(2,128)S(1)}, f32[2,1024]{1,0:T(2,128)}, u32[]{:S(2)}) copy-start(f32[2,1024]{1,0:T(2,128)} %stagger.7) | copy-start | bytes 24580
  65.4 14.2 %copy-start.21 = (f32[2,1024]{1,0:T(2,128)S(1)}, f32[2,1024]{1,0:T(2,128)}, u32[]{:S(2)}) copy-start(f32[2,1024]{1,0:T(2,128)} %area.7) | copy-start | bytes 24580
  71.2 1.1 copy-start.8
  72.2 0.6 copy-start.30
  72.8 14.8 %copy-start.22 = (f32[16,8,128]{2,1,0:T(8,128)}, f32[16,8,128]{2,1,0:T(8,128)S(1)}, u32[]{:S(2)}) copy-start(f32[16,8,128]{2,1,0:T(8,128)S(1)} %get-tuple-element.59.other_in) | copy-start | bytes 196612
  72.8 14.8 %collective-permute-start.8 = (f32[288,128]{1,0:T(8,128)}, f32[288,128]{1,0:T(8,128)S(1)}, u32[]{:S(2)}, u32[]{:S(2)}) collective-permute-start(f32[288,128]{1,0:T(8,128)} %get-tuple-element.56), channel_id=1, source_target_pairs={{0,1},{1,2},{2,3},{4,5},{5,6},{6,7},{8,9},{9,10},{10,11},{12,13},{... | collective-permute-start | bytes 442376 | tf_op jit(solution)/shard_map/ppermute | solution.py:542
  78.0 10.3 %collective-permute-start.9 = (f32[288,128]{1,0:T(8,128)}, f32[288,128]{1,0:T(8,128)}, u32[]{:S(2)}, u32[]{:S(2)}) collective-permute-start(f32[288,128]{1,0:T(8,128)} %get-tuple-element.57), channel_id=1, source_target_pairs={{1,0},{2,1},{3,2},{5,4},{6,5},{7,6},{9,8},{10,9},{11,10},{13,12},{... | collective-permute-start | bytes 442376 | tf_op jit(solution)/shard_map/ppermute | solution.py:543
  79.5 8.8 %copy-start.9 = (f32[288,1024]{1,0:T(8,128)S(1)}, f32[288,1024]{1,0:T(8,128)}, u32[]{:S(2)}) copy-start(f32[288,1024]{1,0:T(8,128)} %copy-done.8) | copy-start | bytes 3538948
  87.6 0.7 copy-start.15
  88.3 2.2 %copy-start.3 = (f32[4,256,1024]{2,1,0:T(8,128)S(1)}, f32[4,256,1024]{2,1,0:T(8,128)}, u32[]{:S(2)}) copy-start(f32[4,256,1024]{2,1,0:T(8,128)} %weights.9) | copy-start | bytes 12582916
  90.5 0.9 copy-start.16
  91.4 0.8 copy-start.23
  92.2 6.1 %copy-start.14 = (bf16[1,120,1024]{2,1,0:T(8,128)(2,1)S(1)}, bf16[1,120,1024]{2,1,0:T(8,128)(2,1)}, u32[]{:S(2)}) copy-start(bf16[1,120,1024]{2,1,0:T(8,128)(2,1)} %refs_8_.1) | copy-start | bytes 737284
  92.2 6.1 %copy-start.27 = (f32[8,1024]{1,0:T(8,128)S(1)}, f32[8,1024]{1,0:T(8,128)}, u32[]{:S(2)}) copy-start(f32[8,1024]{1,0:T(8,128)} %copy-done.26) | copy-start | bytes 98308
  92.2 6.1 %copy-start.29 = (f32[8,1024]{1,0:T(8,128)S(1)}, f32[8,1024]{1,0:T(8,128)}, u32[]{:S(2)}) copy-start(f32[8,1024]{1,0:T(8,128)} %copy-done.28) | copy-start | bytes 98308
  92.2 6.1 %copy-start.31 = (f32[8,1024]{1,0:T(8,128)S(1)}, f32[8,1024]{1,0:T(8,128)}, u32[]{:S(2)}) copy-start(f32[8,1024]{1,0:T(8,128)} %copy-done.30) | copy-start | bytes 98308
  92.2 6.1 %copy-start.32 = (s32[1024]{0:T(1024)S(1)}, s32[1024]{0:T(1024)}, u32[]{:S(2)}) copy-start(s32[1024]{0:T(1024)} %param.27) | copy-start | bytes 12292
where the time goes:
time: 148 us; the launch traced here: 147 us
  blocking collectives  45.3 us (31%)
  Pallas kernels  34.3 us (23%)
  starting transfers between devices  31.5 us (21%)
  local copies, waits for them, and re-layouts  17.8 us (12%)
  waiting for transfers between devices  16.6 us (11%)
    all_to_all x3, blocking collectives, exchanged(): return lax.all_to_all(pieces, axes, 0, 0, tiled=True)  45.3 us
    ppermute x4, starting transfers between devices, on_device(): from_left = lax.ppermute(to_right, 'cell', rightward)  17.7 us
    pallas_call x3, Pallas kernels, next_steps(): pl.pallas_call(functools.partial(next_body, level, tail), out_shape=outs,...  16.9 us
    unnamed x72, local copies, waits for them, and re-layouts  16.5 us
    ppermute x1, waiting for transfers between devices, on_device(): from_mid = lax.ppermute(to_mid, PASS, across)  10.4 us
    ppermute x1, starting transfers between devices, on_device(): from_plane = lax.ppermute(to_plane, PASS, over)  8.54 us
    pallas_call x4, Pallas kernels, kernels(): pl.pallas_call(functools.partial(kernels_body, scale=scale, passages=pass...  8.01 us
    ppermute x4, waiting for transfers between devices, on_device(): from_right = lax.ppermute(to_left, 'cell', leftward)  6.14 us
  transfers between devices with their start and end apart: 10, of which 4 were waited for; matrix products, arithmetic and copies ran while one was open for 0% of the time, Pallas kernels for 5%

commit v1 on v0

--- a/solution.py
+++ b/solution.py
@@ -18,10 +18,12 @@
 WX = W + E
 TOP = 16 + 256
 ROWS = TOP + 16
+PACKED = 24
 SPLIT = {"x": 4, "z": 8, "y_hi": 2}
 PASS = ("x", "z", "y_hi")
-VMEM_LIMIT = 24 * 1024 * 1024
+VMEM_LIMIT = 8 * 1024 * 1024
 F32 = jnp.float32
+EDGE = jax.ShapeDtypeStruct((PACKED, E), F32)
 
 
 def params(**kw):
@@ -65,7 +67,7 @@
 
 
 def strips(field, weights, forcing, lagged, maps):
-    anywhere = pl.BlockSpec(memory_space=pl.ANY)
+    anywhere = pl.BlockSpec(memory_space=pltpu.HBM)
     return pl.pallas_call(
         strips_body,
         out_shape=(jax.ShapeDtypeStruct((48, W), F32), jax.ShapeDtypeStruct((64, W), F32)),
@@ -75,6 +77,29 @@
         compiler_params=params(),
         name="strips",
     )(field, weights, forcing, lagged, maps)
+
+
+def load_body(*refs):
+    count = (len(refs) - 1) // 2
+    copies = [pltpu.make_async_copy(refs[n], refs[count + n], refs[-1].at[n]) for n in range(count)]
+    for copy in copies:
+        copy.start()
+    for copy in copies:
+        copy.wait()
+
+
+def load(arrays):
+    count = len(arrays)
+    return pl.pallas_call(
+        load_body,
+        out_shape=tuple(jax.ShapeDtypeStruct(a.shape, a.dtype) for a in arrays),
+        in_specs=[pl.BlockSpec(memory_space=pltpu.HBM)] * count,
+        out_specs=(vmem(),) * count,
+        scratch_shapes=[pltpu.SemaphoreType.DMA((count,))],
+        compiler_params=params(),
+        cost_estimate=pl.CostEstimate(flops=0, bytes_accessed=12 << 20, transcendentals=0),
+        name="load",
+    )(*arrays)
 
 
 def square(row):
@@ -204,9 +229,26 @@
     return jnp.where(half == 0, plane, mid), jnp.where(half == 0, mid, plane)
 
 
+def packed_edge(block, sign):
+    lane = lax.broadcasted_iota(jnp.int32, (PACKED, E), 1)
+    spot = lane >> 3 if sign == 1 else 15 - (lane >> 3)
+    out = jnp.zeros((PACKED, E), F32)
+    for g in range(ROWS // PACKED):
+        rows = block[PACKED * g : PACKED * (g + 1)]
+        out = jnp.where(spot == g, pltpu.roll(rows, (sign * 8 * g) % E, 1) if g else rows, out)
+    cell = lax.axis_index("cell")
+    end = 0 if sign == 1 else lax.axis_size("cell") - 1
+    return jnp.where(cell == end, 0.0, out)
+
+
+def unpacked_edge(packed, sign):
+    rows = [pltpu.roll(packed, (-sign * 8 * g) % E, 1) if g else packed for g in range(ROWS // PACKED)]
+    return jnp.concatenate(rows, axis=0)
+
+
 def edges_body(
     first, last, u_l, u_r, w_l, w_r, f_l, f_r, lagged, maps, from_mid, from_plane, phase_lag, to_left, to_right,
-    array, own, other,
+    array, own, other, wide,
 ):
     passage, half = place()
     full = slice(0, W)
@@ -232,12 +274,13 @@
                 value = jnp.where(lane == spot, pltpu.roll(e, (sign * (2 + i)) % 128, 1), value)
             return value
 
-        out[16:TOP, :] = packed(u[...], [w[0], w[1], w[2], w[3], f[...]])
+        wide[16:TOP, :] = packed(u[...], [w[0], w[1], w[2], w[3], f[...]])
         pairs = [strip_tiles(from_mid, from_plane, half, 8 * i, lanes) for i in range(6)]
-        out[0:8, :] = packed(pairs[0][0], [p[0] for p in pairs[1:]])
-        out[ROWS - 8 : ROWS, :] = packed(pairs[0][1], [p[1] for p in pairs[1:]])
-        out[8:16, :] = array[8:16, lanes]
-        out[TOP : TOP + 8, :] = array[TOP : TOP + 8, lanes]
+        wide[0:8, :] = packed(pairs[0][0], [p[0] for p in pairs[1:]])
+        wide[ROWS - 8 : ROWS, :] = packed(pairs[0][1], [p[1] for p in pairs[1:]])
+        wide[8:16, :] = array[8:16, lanes]
+        wide[TOP : TOP + 8, :] = array[TOP : TOP + 8, lanes]
+        out[...] = packed_edge(wide[...], sign)
 
 
 def edges(field, weights, forcing, lagged, maps, from_mid, from_plane, phase_lag):
@@ -248,7 +291,7 @@
     return pl.pallas_call(
         edges_body,
         grid=(1,),
-        out_shape=(jax.ShapeDtypeStruct((ROWS, E), F32),) * 2,
+        out_shape=(EDGE,) * 2,
         in_specs=[
             spec((8, W), 0, 0),
             spec((8, W), 31, 0),
@@ -260,16 +303,18 @@
             spec((256, E), 0, 7),
             *whole,
         ],
-        out_specs=(spec((ROWS, E), 0, 0),) * 2,
-        scratch_shapes=[pltpu.VMEM((ROWS, W), F32), pltpu.VMEM((16, 8, 128), F32), pltpu.VMEM((16, 8, 128), F32)],
+        out_specs=(spec((PACKED, E), 0, 0),) * 2,
+        scratch_shapes=[
+            pltpu.VMEM((ROWS, W), F32), pltpu.VMEM((16, 8, 128), F32), pltpu.VMEM((16, 8, 128), F32), pltpu.VMEM((ROWS, E), F32)
+        ],
         compiler_params=params(),
         name="edges",
     )(field, field, field, field, weights, weights, forcing, forcing, lagged, maps, from_mid, from_plane, phase_lag)
 
 
-def set_rim(array, from_left, from_right):
+def set_rim(array, left, right):
     lane = lax.broadcasted_iota(jnp.int32, (ROWS, E), 1)
-    array[:, W:] = jnp.where(lane < 64, from_right[...], from_left[...])
+    array[:, W:] = jnp.where(lane < 64, right, left)
 
 
 def finish(level, source, between, out, surface, weights, forcing, strip, rim, own, other, index, lags, half, tail):
@@ -294,14 +339,15 @@
     source[16:TOP, :W] = field[...]
     source[8:16, :W] = jnp.zeros((8, W), F32)
     source[TOP : TOP + 8, :W] = jnp.zeros((8, W), F32)
-    set_rim(source, from_left, from_right)
+    left_edge, right_edge = unpacked_edge(from_left[...], -1), unpacked_edge(from_right[...], 1)
+    set_rim(source, left_edge, right_edge)
     lane = lax.broadcasted_iota(jnp.int32, (ROWS, E), 1)
     for i in range(5):
         bottom, top = strip_tiles(from_mid, from_plane, half, 8 + 8 * i, full)
         strip[i, 0:8, :] = bottom
         strip[i, 8:16, :] = top
-        right = pltpu.roll(from_right[...], 128 - (2 + i), 1)
-        left = pltpu.roll(from_left[...], 2 + i, 1)
+        right = pltpu.roll(right_edge, 128 - (2 + i), 1)
+        left = pltpu.roll(left_edge, 2 + i, 1)
         rim[i, :, :] = jnp.where(lane == 0, right, jnp.where(lane == 127, left, 0.0))
     keep_lagged(own, lagged.at[0])
     keep_lagged(other, from_plane.at[48:56])
@@ -318,8 +364,8 @@
     between[TOP : TOP + 8, :] = jnp.zeros((8, WX), F32)
     finish(0, source, between, out, surface, weights, forcing, strip, rim, own, other, pair, lags, half, False)
     fill_gaps(out, own, other, pair, lags, half, 2)
-    to_left[...] = out[:, :E]
-    to_right[...] = out[:, W - E :]
+    to_left[...] = packed_edge(out[:, :E], 1)
+    to_right[...] = packed_edge(out[:, W - E :], -1)
 
 
 def next_body(
@@ -333,7 +379,7 @@
     own[...] = own_in[...]
     other[...] = other_in[...]
     source[:, :W] = state[...]
-    set_rim(source, from_left, from_right)
+    set_rim(source, unpacked_edge(from_left[...], -1), unpacked_edge(from_right[...], 1))
     between[8:16, :] = jnp.zeros((8, WX), F32)
     between[TOP : TOP + 8, :] = jnp.zeros((8, WX), F32)
     pair = (index[0:8, :], index[8:16, :])
@@ -343,12 +389,11 @@
         out[8:16, :] = jnp.zeros((8, W), F32)
         out[TOP : TOP + 8, :] = jnp.zeros((8, W), F32)
         fill_gaps(out, own, other, pair, lags, half, level + 2)
-        to_left[...] = out[:, :E]
-        to_right[...] = out[:, W - E :]
+        to_left[...] = packed_edge(out[:, :E], 1)
+        to_right[...] = packed_edge(out[:, W - E :], -1)
 
 
 HISTORY = jax.ShapeDtypeStruct((16, 8, 128), F32)
-EDGE = jax.ShapeDtypeStruct((ROWS, E), F32)
 STATE = jax.ShapeDtypeStruct((ROWS, W), F32)
 BUFFERS = [pltpu.VMEM((ROWS, WX), F32), pltpu.VMEM((ROWS, WX), F32)]
 COST = pl.CostEstimate(flops=2 * 16 * 330 * 1024, bytes_accessed=8 << 20, transcendentals=0)
@@ -515,19 +560,23 @@
     scale = 64.0 / math.sqrt(W * cells * passes)
     across = [(i, i ^ 1) for i in range(passes)]
     over = [(i, ((i + 1) ^ 1) - 1 if 0 < i < passes - 1 else passes - 1 - i) for i in range(passes)]
-    rightward = [(i, i + 1) for i in range(cells - 1)]
-    leftward = [(i + 1, i) for i in range(cells - 1)]
-
-    to_mid, to_plane = strips(flow_state, face_weights, forcing, lagged_planes, face_map)
+    rightward = [(i, (i + 1) % cells) for i in range(cells)]
+    leftward = [(j, i) for i, j in rightward]
+
+    far = (flow_state, face_weights, forcing, lagged_planes)
+    to_mid, to_plane = strips(*[pltpu.with_memory_space_constraint(x, pltpu.HBM) for x in far], face_map)
+    points, to_mid, to_plane, far = lax.optimization_barrier((listeners.T, to_mid, to_plane, far[:3]))
     from_mid = lax.ppermute(to_mid, PASS, across)
     from_plane = lax.ppermute(to_plane, PASS, over)
 
-    points = listeners.T
     pairs = [
         kernels(points, face_radius, face_angle, face_axial, face_stagger, face_area, n, 4, scale, passes // 2)
         for n in range(4)
     ]
 
+    near = load([pltpu.with_memory_space_constraint(x, pltpu.HBM) for x in far])
+    pairs, near, from_mid, from_plane = lax.optimization_barrier((pairs, near, from_mid, from_plane))
+    flow_state, face_weights, forcing = [pltpu.with_memory_space_constraint(x, pltpu.VMEM) for x in near]
     to_left, to_right = edges(
         flow_state, face_weights, forcing, lagged_planes, face_map, from_mid, from_plane, phase_lag
     )

time: 148 us -> 108 us (0.73)
  starting transfers between devices: 31.5 us -> 16 us
  local copies, waits for them, and re-layouts: 17.8 us -> 3.04 us
  waiting for transfers between devices: 16.6 us -> 5.62 us
  Pallas kernels: 34.3 us -> 37.3 us
    ppermute x4, starting transfers between devices: 17.7 us -> 2.6 us  [on_device(): from_left = lax.ppermute(to_right, 'cell', rightward)]
    unnamed x72 -> x24, local copies, waits for them, and re-layouts: 16.5 us -> 1.75 us
    ppermute x1, waiting for transfers between devices: 10.4 us -> 0.01 us  [on_device(): from_mid = lax.ppermute(to_mid, PASS, across)]
    ppermute x4, waiting for transfers between devices: 6.14 us -> 0.3 us  [on_device(): from_right = lax.ppermute(to_left, 'cell', leftward)]
    ppermute x4, waiting for transfers between devices: 0.01 us -> 5.31 us  [on_device(): from_left = lax.ppermute(to_right, 'cell', rightward)]
    pallas_call x1 -> x2, Pallas kernels: 1.54 us -> 4.55 us  [the longest x1 2.86 us: load(): pl.pallas_call(load_body, out_shape=tuple((jax.ShapeDtypeStruct(a.shape,...]
  transfers between devices with their start and end apart: 10 -> 10, of which waited for: 4 -> 7; matrix products, arithmetic and copies ran while one was open for 0% -> 0% of each run, Pallas kernels for 5% -> 10%
where the time goes in v1:
time: 108 us; the launch traced here: 107 us
  blocking collectives  44.3 us (41%)
  Pallas kernels  37.3 us (35%)
  starting transfers between devices  16 us (15%)
  waiting for transfers between devices  5.62 us (5%)
  local copies, waits for them, and re-layouts  3.04 us (3%)
    all_to_all x3, blocking collectives, exchanged(): return lax.all_to_all(pieces, axes, 0, 0, tiled=True)  44.3 us
    pallas_call x3, Pallas kernels, next_steps(): pl.pallas_call(functools.partial(next_body, level, tail), out_shape=outs,...  16.4 us
    ppermute x1, starting transfers between devices, on_device(): from_plane = lax.ppermute(to_plane, PASS, over)  8.54 us
    pallas_call x4, Pallas kernels, kernels(): pl.pallas_call(functools.partial(kernels_body, scale=scale, passages=pass...  8.01 us
    pallas_call x1, Pallas kernels, first_steps(): pl.pallas_call(first_body, out_shape=outs, in_specs=[vmem()] * 9 + [smem(...  5.79 us
    ppermute x4, waiting for transfers between devices, on_device(): from_left = lax.ppermute(to_right, 'cell', rightward)  5.31 us
    ppermute x4, starting transfers between devices, on_device(): from_right = lax.ppermute(to_left, 'cell', leftward)  4.86 us
    pallas_call x1, Pallas kernels, load(): pl.pallas_call(load_body, out_shape=tuple((jax.ShapeDtypeStruct(a.shape,...  2.86 us
  transfers between devices with their start and end apart: 10, of which 7 were waited for; matrix products, arithmetic and copies ran while one was open for 0% of the time, Pallas kernels for 10%

profile of v1, /device:TPU:2, one launch (start us, length us, event | category | flops | bytes accessed | tf_op | source)
XLA Modules:
  0.0 107.2 jit_solution(17896030537752288312)
XLA Ops:
  0.6 0.9 copy.23
  1.6 0.0 copy-start.7
  1.6 0.7 copy-done.7
  2.3 1.1 %strips.1 = (f32[48,1024]{1,0:T(8,128)S(1)}, f32[64,1024]{1,0:T(8,128)S(1)}) custom-call(f32[256,1024]{1,0:T(8,128)} %refs_0_, f32[4,256,1024]{2,1,0:T(8,128)} %refs_1_, f32[256,1024]{1,0:T(8,128)} %refs_2_, f32[1,8,1024]{2,1,0:T(8,128)} %lagged.5, s32[1,1024]{1,0:T(1,128)S(1)} %copy-done.7), custom_call_target="tpu_custom_call" | custom-call | tf_op jit(solution)/shard_map/strips/pallas_call | solution.py:71
  3.3 8.5 %collective-permute-start.1 = (f32[64,1024]{1,0:T(8,128)S(1)}, f32[64,1024]{1,0:T(8,128)S(1)}, u32[]{:S(2)}, u32[]{:S(2)}) collective-permute-start(f32[64,1024]{1,0:T(8,128)S(1)} %get-tuple-element.78), channel_id=1, source_target_pairs={{0,252},{4,8},{8,4},{12,16},{16,12},{20,24},{24,20},{28,32},{32,28... | collective-permute-start | bytes 786440 | tf_op jit(solution)/shard_map/ppermute | solution.py:570
  11.9 0.0 collective-permute-start
  11.9 0.0 copy-done.10
  11.9 0.1 copy.24.phase_lag
  12.0 0.0 copy-start.5
  12.0 0.0 copy-start.6
  12.0 2.9 %load.1 = (f32[256,1024]{1,0:T(8,128)S(1)}, f32[4,256,1024]{2,1,0:T(8,128)S(1)}, f32[256,1024]{1,0:T(8,128)S(1)}) custom-call(f32[256,1024]{1,0:T(8,128)} %refs_0_, f32[4,256,1024]{2,1,0:T(8,128)} %refs_1_, f32[256,1024]{1,0:T(8,128)} %refs_2_), custom_call_target="tpu_custom_call" | custom-call | bytes 12582912 | tf_op jit(solution)/shard_map/load/pallas_call | solution.py:93
  14.9 0.0 copy-start
  14.9 0.0 copy-start.8
  15.0 2.0 %kernels_3.1 = (bf16[256,1024]{1,0:T(8,128)(2,1)S(1)}, bf16[256,1024]{1,0:T(8,128)(2,1)S(1)}) custom-call(f32[1024,3]{1,0:T(8,128)S(1)} %bitcast.4, f32[2,1024]{1,0:T(2,128)S(1)} %copy-done.2, f32[2,1024]{1,0:T(2,128)S(1)} %copy-done.3, f32[2,1024]{1,0:T(2,128)S(1)} %copy-done.4, f32[2,1024]{1,0:T(2,128)S(1)} %copy-done.5, f32[2,1024]{1,0:T(2,128)S(1)} %copy-done.6), custom_call_target="tpu_custom_call" | custom-call | flops 5242880 | bytes 1048576 | tf_op jit(solution)/shard_map/kernels_3/pallas_call | solution.py:478
  17.0 2.0 %kernels_2.1 = (bf16[256,1024]{1,0:T(8,128)(2,1)S(1)}, bf16[256,1024]{1,0:T(8,128)(2,1)S(1)}) custom-call(f32[1024,3]{1,0:T(8,128)S(1)} %bitcast.5, f32[2,1024]{1,0:T(2,128)S(1)} %copy-done.2, f32[2,1024]{1,0:T(2,128)S(1)} %copy-done.3, f32[2,1024]{1,0:T(2,128)S(1)} %copy-done.4, f32[2,1024]{1,0:T(2,128)S(1)} %copy-done.5, f32[2,1024]{1,0:T(2,128)S(1)} %copy-done.6), custom_call_target="tpu_custom_call" | custom-call | flops 5242880 | bytes 1048576 | tf_op jit(solution)/shard_map/kernels_2/pallas_call | solution.py:478
  19.0 2.0 %kernels_1.1 = (bf16[256,1024]{1,0:T(8,128)(2,1)S(1)}, bf16[256,1024]{1,0:T(8,128)(2,1)S(1)}) custom-call(f32[1024,3]{1,0:T(8,128)S(1)} %bitcast.6, f32[2,1024]{1,0:T(2,128)S(1)} %copy-done.2, f32[2,1024]{1,0:T(2,128)S(1)} %copy-done.3, f32[2,1024]{1,0:T(2,128)S(1)} %copy-done.4, f32[2,1024]{1,0:T(2,128)S(1)} %copy-done.5, f32[2,1024]{1,0:T(2,128)S(1)} %copy-done.6), custom_call_target="tpu_custom_call" | custom-call | flops 5242880 | bytes 1048576 | tf_op jit(solution)/shard_map/kernels_1/pallas_call | solution.py:478
  21.0 2.0 %kernels_0.1 = (bf16[256,1024]{1,0:T(8,128)(2,1)S(1)}, bf16[256,1024]{1,0:T(8,128)(2,1)S(1)}) custom-call(f32[1024,3]{1,0:T(8,128)S(1)} %bitcast.7, f32[2,1024]{1,0:T(2,128)S(1)} %copy-done.2, f32[2,1024]{1,0:T(2,128)S(1)} %copy-done.3, f32[2,1024]{1,0:T(2,128)S(1)} %copy-done.4, f32[2,1024]{1,0:T(2,128)S(1)} %copy-done.5, f32[2,1024]{1,0:T(2,128)S(1)} %copy-done.6), custom_call_target="tpu_custom_call" | custom-call | flops 5242880 | bytes 1048576 | tf_op jit(solution)/shard_map/kernels_0/pallas_call | solution.py:478
  23.0 0.0 collective-permute-done.from_mid
  23.0 0.0 collective-permute-done.1.from_plane
  23.0 1.7 %edges.1 = (f32[24,128]{1,0:T(8,128)S(1)}, f32[24,128]{1,0:T(8,128)S(1)}) custom-call(f32[256,1024]{1,0:T(8,128)S(1)} %get-tuple-element.79.first.last.u_l.u_r.field, f32[256,1024]{1,0:T(8,128)S(1)} %get-tuple-element.79.first.last.u_l.u_r.field, f32[256,1024]{1,0:T(8,128)S(1)} %get-tuple-element.79.first.last.u_l.u_r.field, ...), custom_call_target="tpu_custom_call" | custom-call | tf_op jit(solution)/shard_map/edges/pallas_call | solution.py:291
  24.7 0.1 collective-permute-start.2
  24.8 1.7 %collective-permute-start.3 = (f32[24,128]{1,0:T(8,128)S(1)}, f32[24,128]{1,0:T(8,128)S(1)}, u32[]{:S(2)}, u32[]{:S(2)}) collective-permute-start(f32[24,128]{1,0:T(8,128)S(1)} %get-tuple-element.85), channel_id=1, source_target_pairs={{1,0},{2,1},{3,2},{0,3},{5,4},{6,5},{7,6},{4,7},{9,8},{10,9},{11,1... | collective-permute-start | bytes 36872 | tf_op jit(solution)/shard_map/ppermute | solution.py:584
  26.6 1.4 %collective-permute-done.2.from_left = f32[24,128]{1,0:T(8,128)S(1)} collective-permute-done((f32[24,128]{1,0:T(8,128)S(1)}, f32[24,128]{1,0:T(8,128)S(1)}, u32[]{:S(2)}, u32[]{:S(2)}) %collective-permute-start.2) | collective-permute-done | bytes 12320 | tf_op jit(solution)/shard_map/ppermute | solution.py:583
  27.9 0.0 collective-permute-done.3.from_right
  28.0 5.8 %steps_first.1 = (f32[288,1024]{1,0:T(8,128)S(1)}, f32[24,128]{1,0:T(8,128)S(1)}, f32[24,128]{1,0:T(8,128)S(1)}, f32[8,1024]{1,0:T(8,128)S(1)}, f32[16,8,128]{2,...) custom-call(f32[256,1024]{1,0:T(8,128)S(1)} %get-tuple-element.79.fi, ...), custom_call_target="tpu_custom_call" | custom-call | flops 10813440 | bytes 8388608 | tf_op jit(solution)/shard_map/steps_first/pallas_call | solution.py:408
  33.8 0.8 collective-permute-start.4
  34.6 1.0 collective-permute-start.5
  35.6 1.3 %collective-permute-done.4.from_left = f32[24,128]{1,0:T(8,128)S(1)} collective-permute-done((f32[24,128]{1,0:T(8,128)S(1)}, f32[24,128]{1,0:T(8,128)S(1)}, u32[]{:S(2)}, u32[]{:S(2)}) %collective-permute-start.4) | collective-permute-done | bytes 12320 | tf_op jit(solution)/shard_map/ppermute | solution.py:591
  37.0 0.1 collective-permute-done.5.from_right
  37.0 5.2 %steps_2.1 = (f32[288,1024]{1,0:T(8,128)S(1)}, f32[24,128]{1,0:T(8,128)S(1)}, f32[24,128]{1,0:T(8,128)S(1)}, f32[8,1024]{1,0:T(8,128)S(1)}, f32[16,8,128]{2,1,0:T(8,128)S(1)}, /*index=5*/f32[16,8,128]{2,1,0:T(8,128)S(1)}) custom-call(f32[288,1024]{1,0:T(8,128)S(1)} %get-tuple-element.86.state, f32[4,256,1024]{2,1,0:T(8,128)S(1)} %get-tuple-element.80.w_l.w_r.weights, ...), custom_call_target="tpu_custom_call" | custom-call | flops 10813440 | bytes 8388608 | tf_op jit(solution)/shard_map/steps_2/pallas_call | solution.py:429
  42.3 0.8 collective-permute-start.6
  43.1 1.0 collective-permute-start.7
  44.2 1.3 %collective-permute-done.6.from_left = f32[24,128]{1,0:T(8,128)S(1)} collective-permute-done((f32[24,128]{1,0:T(8,128)S(1)}, f32[24,128]{1,0:T(8,128)S(1)}, u32[]{:S(2)}, u32[]{:S(2)}) %collective-permute-start.6) | collective-permute-done | bytes 12320 | tf_op jit(solution)/shard_map/ppermute | solution.py:591
  45.5 0.1 collective-permute-done.7.from_right
  45.6 5.2 %steps_4.1 = (f32[288,1024]{1,0:T(8,128)S(1)}, f32[24,128]{1,0:T(8,128)S(1)}, f32[24,128]{1,0:T(8,128)S(1)}, f32[8,1024]{1,0:T(8,128)S(1)}, f32[16,8,128]{2,1,0:T(8,128)S(1)}, /*index=5*/f32[16,8,128]{2,1,0:T(8,128)S(1)}) custom-call(f32[288,1024]{1,0:T(8,128)S(1)} %get-tuple-element.94.state, f32[4,256,1024]{2,1,0:T(8,128)S(1)} %get-tuple-element.80.w_l.w_r.weights, ...), custom_call_target="tpu_custom_call" | custom-call | flops 10813440 | bytes 8388608 | tf_op jit(solution)/shard_map/steps_4/pallas_call | solution.py:429
  50.8 0.8 collective-permute-start.8
  51.6 1.0 collective-permute-start.9
  52.7 1.3 %collective-permute-done.8.from_left = f32[24,128]{1,0:T(8,128)S(1)} collective-permute-done((f32[24,128]{1,0:T(8,128)S(1)}, f32[24,128]{1,0:T(8,128)S(1)}, u32[]{:S(2)}, u32[]{:S(2)}) %collective-permute-start.8) | collective-permute-done | bytes 12320 | tf_op jit(solution)/shard_map/ppermute | solution.py:591
  54.0 0.1 collective-permute-done.9.from_right
  54.1 5.9 %steps_6.1 = (f32[256,1024]{1,0:T(8,128)}, f32[8,1024]{1,0:T(8,128)S(1)}) custom-call(f32[288,1024]{1,0:T(8,128)S(1)} %get-tuple-element.99.state, f32[4,256,1024]{2,1,0:T(8,128)S(1)} %get-tuple-element.80.w_l.w_r.weights, f32[256,1024]{1,0:T(8,128)S(1)} %get-tuple-element.81.f_l.f_r.forcing, f32[24,128]{1,0:T(8,128)S(1)} %collective-permute-done.8.from_left, ...), custom_call_target="tpu_custom_call" | custom-call | flops 10813440 | bytes 8388608 | tf_op jit(solution)/shard_map/steps_6/pallas_call | solution.py:429
  60.0 0.0 copy-done.9
  60.0 1.5 %sound.1 = f32[32,40,128]{2,1,0:T(8,128)S(1)} custom-call(bf16[256,1024]{1,0:T(8,128)(2,1)S(1)} %get-tuple-element.105.refs_0_, bf16[256,1024]{1,0:T(8,128)(2,1)S(1)} %get-tuple-element.106.refs_1_, bf16[256,1024]{1,0:T(8,128)(2,1)S(1)} %get-tuple-element.107.refs_2_, bf16[256,1024]{1,0:T(8,128)(2,1)S(1)} %get-tuple-element.108.refs_3_, ...), custom_call_target="tpu_custom_call" | custom-call | tf_op jit(solution)/shard_map/sound/pallas_call | solution.py:522
  61.5 19.6 %all_to_all.15 = f32[32,40,128]{2,1,0:T(8,128)S(1)} all-to-all(f32[32,40,128]{2,1,0:T(8,128)S(1)} %sound.1), channel_id=1, replica_groups=mesh['x'=4,'z'=8,'y_hi'=2,'cell'=4] {'x','y_hi','cell'}, dimensions={0} | all-to-all | bytes 1310720 | tf_op jit(solution)/shard_map/all_to_all | solution.py:534
  81.2 0.1 reduce_sum.18
  81.2 13.8 %all_to_all.16 = f32[8,40,128]{2,1,0:T(8,128)S(1)} all-to-all(f32[8,40,128]{2,1,0:T(8,128)S(1)} %broadcast_in_dim.10), channel_id=1, replica_groups=mesh['x'=4,'z'=8,'y_hi'=2,'cell'=4] {'z'}, dimensions={0} | all-to-all | bytes 327680 | tf_op jit(solution)/shard_map/all_to_all | solution.py:534
  95.1 10.8 %all_to_all.17 = f32[8,40,128]{2,1,0:T(8,128)S(1)} all-to-all(f32[8,40,128]{2,1,0:T(8,128)S(1)} %broadcast_in_dim.11), channel_id=1, replica_groups=mesh['x'=4,'z'=8,'y_hi'=2,'cell'=4] {'x','y_hi'}, dimensions={0} | all-to-all | bytes 327680 | tf_op jit(solution)/shard_map/all_to_all | solution.py:534
  105.9 0.6 slice.9
  106.5 0.7 slice.8
  (17 shorter events, 0.1 us)
Async XLA Ops:
  1.6 0.7 copy-start.7
  2.3 9.6 %copy-start.10 = (s32[32,2]{0,1:T(2,128)S(1)}, s32[32,2]{0,1:T(2,128)}, u32[]{:S(2)}) copy-start(s32[32,2]{0,1:T(2,128)} %param.18) | copy-start | bytes 772
  3.3 19.7 %collective-permute-start.1 = (f32[64,1024]{1,0:T(8,128)S(1)}, f32[64,1024]{1,0:T(8,128)S(1)}, u32[]{:S(2)}, u32[]{:S(2)}) collective-permute-start(f32[64,1024]{1,0:T(8,128)S(1)} %get-tuple-element.78), channel_id=1, source_target_pairs={{0,252},{4,8},{8,4},{12,16},{16,12},{20,24},{24,20},{28,32},{32,28... | collective-permute-start | bytes 786440 | tf_op jit(solution)/shard_map/ppermute | solution.py:570
  11.9 11.1 %collective-permute-start = (f32[48,1024]{1,0:T(8,128)S(1)}, f32[48,1024]{1,0:T(8,128)S(1)}, u32[]{:S(2)}, u32[]{:S(2)}) collective-permute-start(f32[48,1024]{1,0:T(8,128)S(1)} %get-tuple-element.77), channel_id=1, source_target_pairs={{0,4},{4,0},{8,12},{12,8},{16,20},{20,16},{24,28},{28,24},{32,36},... | collective-permute-start | bytes 589832 | tf_op jit(solution)/shard_map/ppermute | solution.py:569
  12.0 2.9 %copy-start.2 = (f32[2,1024]{1,0:T(2,128)S(1)}, f32[2,1024]{1,0:T(2,128)}, u32[]{:S(2)}) copy-start(f32[2,1024]{1,0:T(2,128)} %radius.7) | copy-start | bytes 24580
  12.0 2.9 %copy-start.3 = (f32[2,1024]{1,0:T(2,128)S(1)}, f32[2,1024]{1,0:T(2,128)}, u32[]{:S(2)}) copy-start(f32[2,1024]{1,0:T(2,128)} %angle.7) | copy-start | bytes 24580
  12.0 2.9 %copy-start.4 = (f32[2,1024]{1,0:T(2,128)S(1)}, f32[2,1024]{1,0:T(2,128)}, u32[]{:S(2)}) copy-start(f32[2,1024]{1,0:T(2,128)} %axial.7) | copy-start | bytes 24580
  12.0 2.9 %copy-start.5 = (f32[2,1024]{1,0:T(2,128)S(1)}, f32[2,1024]{1,0:T(2,128)}, u32[]{:S(2)}) copy-start(f32[2,1024]{1,0:T(2,128)} %stagger.7) | copy-start | bytes 24580
  12.0 2.9 %copy-start.6 = (f32[2,1024]{1,0:T(2,128)S(1)}, f32[2,1024]{1,0:T(2,128)}, u32[]{:S(2)}) copy-start(f32[2,1024]{1,0:T(2,128)} %area.7) | copy-start | bytes 24580
  14.9 8.1 %copy-start = (f32[1,8,1024]{2,1,0:T(8,128)S(1)}, f32[1,8,1024]{2,1,0:T(8,128)}, u32[]{:S(2)}) copy-start(f32[1,8,1024]{2,1,0:T(8,128)} %lagged.5) | copy-start | bytes 98308
  14.9 8.1 %copy-start.8 = (s32[1,1024]{1,0:T(1,128)S(1)}, s32[1,1024]{1,0:T(1,128)}, u32[]{:S(2)}) copy-start(s32[1,1024]{1,0:T(1,128)} %maps.5) | copy-start | bytes 12292
  24.7 3.2 %collective-permute-start.2 = (f32[24,128]{1,0:T(8,128)S(1)}, f32[24,128]{1,0:T(8,128)S(1)}, u32[]{:S(2)}, u32[]{:S(2)}) collective-permute-start(f32[24,128]{1,0:T(8,128)S(1)} %get-tuple-element.84), channel_id=1, source_target_pairs={{0,1},{1,2},{2,3},{3,0},{4,5},{5,6},{6,7},{7,4},{8,9},{9,10},{10,1... | collective-permute-start | bytes 36872 | tf_op jit(solution)/shard_map/ppermute | solution.py:583
  24.8 3.1 %collective-permute-start.3 = (f32[24,128]{1,0:T(8,128)S(1)}, f32[24,128]{1,0:T(8,128)S(1)}, u32[]{:S(2)}, u32[]{:S(2)}) collective-permute-start(f32[24,128]{1,0:T(8,128)S(1)} %get-tuple-element.85), channel_id=1, source_target_pairs={{1,0},{2,1},{3,2},{0,3},{5,4},{6,5},{7,6},{4,7},{9,8},{10,9},{11,1... | collective-permute-start | bytes 36872 | tf_op jit(solution)/shard_map/ppermute | solution.py:584
  33.8 3.2 %collective-permute-start.4 = (f32[24,128]{1,0:T(8,128)S(1)}, f32[24,128]{1,0:T(8,128)S(1)}, u32[]{:S(2)}, u32[]{:S(2)}) collective-permute-start(f32[24,128]{1,0:T(8,128)S(1)} %get-tuple-element.87), channel_id=1, source_target_pairs={{0,1},{1,2},{2,3},{3,0},{4,5},{5,6},{6,7},{7,4},{8,9},{9,10},{10,1... | collective-permute-start | bytes 36872 | tf_op jit(solution)/shard_map/ppermute | solution.py:591
  34.6 2.4 %collective-permute-start.5 = (f32[24,128]{1,0:T(8,128)S(1)}, f32[24,128]{1,0:T(8,128)S(1)}, u32[]{:S(2)}, u32[]{:S(2)}) collective-permute-start(f32[24,128]{1,0:T(8,128)S(1)} %get-tuple-element.88), channel_id=1, source_target_pairs={{1,0},{2,1},{3,2},{0,3},{5,4},{6,5},{7,6},{4,7},{9,8},{10,9},{11,1... | collective-permute-start | bytes 36872 | tf_op jit(solution)/shard_map/ppermute | solution.py:592
  42.3 3.2 %collective-permute-start.6 = (f32[24,128]{1,0:T(8,128)S(1)}, f32[24,128]{1,0:T(8,128)S(1)}, u32[]{:S(2)}, u32[]{:S(2)}) collective-permute-start(f32[24,128]{1,0:T(8,128)S(1)} %get-tuple-element.95), channel_id=1, source_target_pairs={{0,1},{1,2},{2,3},{3,0},{4,5},{5,6},{6,7},{7,4},{8,9},{9,10},{10,1... | collective-permute-start | bytes 36872 | tf_op jit(solution)/shard_map/ppermute | solution.py:591
  43.1 2.4 %collective-permute-start.7 = (f32[24,128]{1,0:T(8,128)S(1)}, f32[24,128]{1,0:T(8,128)S(1)}, u32[]{:S(2)}, u32[]{:S(2)}) collective-permute-start(f32[24,128]{1,0:T(8,128)S(1)} %get-tuple-element.96), channel_id=1, source_target_pairs={{1,0},{2,1},{3,2},{0,3},{5,4},{6,5},{7,6},{4,7},{9,8},{10,9},{11,1... | collective-permute-start | bytes 36872 | tf_op jit(solution)/shard_map/ppermute | solution.py:592
  50.8 3.2 %collective-permute-start.8 = (f32[24,128]{1,0:T(8,128)S(1)}, f32[24,128]{1,0:T(8,128)S(1)}, u32[]{:S(2)}, u32[]{:S(2)}) collective-permute-start(f32[24,128]{1,0:T(8,128)S(1)} %get-tuple-element.100), channel_id=1, source_target_pairs={{0,1},{1,2},{2,3},{3,0},{4,5},{5,6},{6,7},{7,4},{8,9},{9,10},{10,1... | collective-permute-start | bytes 36872 | tf_op jit(solution)/shard_map/ppermute | solution.py:591
  51.6 2.4 %collective-permute-start.9 = (f32[24,128]{1,0:T(8,128)S(1)}, f32[24,128]{1,0:T(8,128)S(1)}, u32[]{:S(2)}, u32[]{:S(2)}) collective-permute-start(f32[24,128]{1,0:T(8,128)S(1)} %get-tuple-element.101), channel_id=1, source_target_pairs={{1,0},{2,1},{3,2},{0,3},{5,4},{6,5},{7,6},{4,7},{9,8},{10,9},{11,1... | collective-permute-start | bytes 36872 | tf_op jit(solution)/shard_map/ppermute | solution.py:592
  54.1 5.9 %copy-start.1 = (bf16[1,120,1024]{2,1,0:T(8,128)(2,1)S(1)}, bf16[1,120,1024]{2,1,0:T(8,128)(2,1)}, u32[]{:S(2)}) copy-start(bf16[1,120,1024]{2,1,0:T(8,128)(2,1)} %refs_8_.1) | copy-start | bytes 737284
  54.1 5.9 %copy-start.9 = (s32[1024]{0:T(1024)S(1)}, s32[1024]{0:T(1024)}, u32[]{:S(2)}) copy-start(s32[1024]{0:T(1024)} %param.27) | copy-start | bytes 12292

commit v2 on v1

--- a/solution.py
+++ b/solution.py
@@ -24,6 +24,9 @@
 VMEM_LIMIT = 8 * 1024 * 1024
 F32 = jnp.float32
 EDGE = jax.ShapeDtypeStruct((PACKED, E), F32)
+HISTORY = jax.ShapeDtypeStruct((16, 8, 128), F32)
+INDEX = jax.ShapeDtypeStruct((32, 128), jnp.int32)
+GAPS = jax.ShapeDtypeStruct((16, W), F32)
 
 
 def params(**kw):
@@ -32,10 +35,6 @@
 
 def vmem():
     return pl.BlockSpec(memory_space=pltpu.VMEM)
-
-
-def smem():
-    return pl.BlockSpec(memory_space=pltpu.SMEM)
 
 
 def place():
@@ -44,7 +43,7 @@
     return index // 2, index % 2
 
 
-def strips_body(field, weights, forcing, lagged, maps, to_mid, to_plane, sems):
+def strips_body(field, weights, forcing, lagged, maps, to_mid, to_plane, row, sems):
     _, half = place()
     mid = pl.multiple_of(jnp.where(half == 0, 248, 0), 8)
     plane = pl.multiple_of(jnp.where(half == 0, 0, 248), 8)
@@ -56,14 +55,15 @@
             copies.append((weights.at[i, rows], out.at[pl.ds(8 + 8 * i, 8)]))
         copies.append((forcing.at[rows], out.at[pl.ds(40, 8)]))
     copies.append((lagged.at[0], to_plane.at[pl.ds(48, 8)]))
+    copies.append((maps, row))
     started = []
     for n, (source, target) in enumerate(copies):
         copy = pltpu.make_async_copy(source, target, sems.at[n])
         copy.start()
         started.append(copy)
-    to_plane[56:64, :] = jnp.broadcast_to(maps[...].astype(F32), (8, W))
     for copy in started:
         copy.wait()
+    to_plane[56:64, :] = jnp.broadcast_to(row[...].astype(F32), (8, W))
 
 
 def strips(field, weights, forcing, lagged, maps):
@@ -71,9 +71,9 @@
     return pl.pallas_call(
         strips_body,
         out_shape=(jax.ShapeDtypeStruct((48, W), F32), jax.ShapeDtypeStruct((64, W), F32)),
-        in_specs=[anywhere, anywhere, anywhere, anywhere, vmem()],
+        in_specs=[anywhere] * 5,
         out_specs=(vmem(), vmem()),
-        scratch_shapes=[pltpu.SemaphoreType.DMA((13,))],
+        scratch_shapes=[pltpu.VMEM((1, W), jnp.int32), pltpu.SemaphoreType.DMA((14,))],
         compiler_params=params(),
         name="strips",
     )(field, weights, forcing, lagged, maps)
@@ -107,14 +107,13 @@
     return jnp.concatenate(tiles, axis=0).astype(jnp.int32) & (W - 1)
 
 
-def level_row(level):
-    return jnp.where(level >= 0, 8 + level, -level - 1)
-
-
-def picked(history, level, index):
-    row = level_row(level)
+def picked(history, level, lag, index):
+    back = level - lag
+    row = jnp.where(back >= 0, 8 + back, -back - 1)
+    tiles = history[0]
+    for n in range(1, 9 + level):
+        tiles = jnp.where(row == n, history[n], tiles)
     high, low = index >> 7, index & 127
-    tiles = history[row]
     out = jnp.zeros((8, 128), F32)
     for b in range(8):
         source = jnp.broadcast_to(tiles[b : b + 1, :], (8, 128))
@@ -123,57 +122,43 @@
     return out
 
 
-def keep_row(history, row, array, at):
-    for b in range(8):
-        history[row, b : b + 1, :] = array[at : at + 1, 128 * b : 128 * (b + 1)]
-
-
 def keep_lagged(history, lagged):
     for j in range(8):
         for b in range(8):
             history[j, b : b + 1, :] = lagged[j : j + 1, 128 * b : 128 * (b + 1)]
 
 
-def put_row(array, row, value):
-    for s in range(8):
-        array[row : row + 1, 128 * s : 128 * (s + 1)] = value[s : s + 1, :]
-
-
-def fill_gaps(array, own, other, index, lags, half, level):
-    main = pl.ds(0, W)
-
-    @pl.when(half == 0)
-    def _():
-        keep_row(own, 8 + level, array, 16)
-        keep_row(other, 8 + level, array, 7)
-
-    @pl.when(half == 1)
-    def _():
-        keep_row(own, 8 + level, array, TOP - 1)
-        keep_row(other, 8 + level, array, TOP + 8)
-
-    mine = picked(other, level - lags[0], index[0])
-    theirs = picked(own, level - lags[1], index[1])
-
-    @pl.when(half == 0)
-    def _():
-        put_row(array, 15, mine)
-        put_row(array, 8, theirs)
-        array[TOP : TOP + 1, main] = array[TOP + 8 : TOP + 9, main]
-        array[TOP + 7 : TOP + 8, main] = array[TOP - 1 : TOP, main]
-
-    @pl.when(half == 1)
-    def _():
-        put_row(array, TOP, mine)
-        put_row(array, TOP + 7, theirs)
-        array[15:16, main] = array[7:8, main]
-        array[8:9, main] = array[16:17, main]
-
-
-def lag_pair(phase_lag, passage, half):
+def fill_gaps(array, own, other, index, half, level):
+    low = half == 0
+    lanes = [slice(128 * b, 128 * (b + 1)) for b in range(8)]
+    ends = [[array[r : r + 1, k] for k in lanes] for r in (7, 16, TOP - 1, TOP + 8)]
+    for b in range(8):
+        own[8 + level, b : b + 1, :] = jnp.where(low, ends[1][b], ends[2][b])
+        other[8 + level, b : b + 1, :] = jnp.where(low, ends[0][b], ends[3][b])
+    mine = picked(other, level, index[16:24, :], index[0:8, :])
+    theirs = picked(own, level, index[24:32, :], index[8:16, :])
+    for b, k in enumerate(lanes):
+        array[15:16, k] = jnp.where(low, mine[b : b + 1], ends[0][b])
+        array[8:9, k] = jnp.where(low, theirs[b : b + 1], ends[1][b])
+        array[TOP : TOP + 1, k] = jnp.where(low, ends[3][b], mine[b : b + 1])
+        array[TOP + 7 : TOP + 8, k] = jnp.where(low, ends[2][b], theirs[b : b + 1])
+
+
+def lag_square(phase_lag, row, column):
+    count, sides = phase_lag.shape
+    at = lax.broadcasted_iota(jnp.int32, (count, sides), 0) == row
+    at = at & (lax.broadcasted_iota(jnp.int32, (count, sides), 1) == column)
+    lag = jnp.sum(jnp.where(at, phase_lag[...].astype(F32), 0.0), axis=0, keepdims=True)
+    lag = jnp.sum(lag, axis=1, keepdims=True)
+    return jnp.broadcast_to(lag, (8, 128)).astype(jnp.int32)
+
+
+def set_index(index, maps, other_maps, phase_lag, passage, half):
     count = phase_lag.shape[0]
-    beside = lax.rem(passage + 2 * half - 1 + count, count)
-    return phase_lag[passage, half], phase_lag[beside, 1 - half]
+    index[0:8, :] = square(maps)
+    index[8:16, :] = square(other_maps)
+    index[16:24, :] = lag_square(phase_lag, passage, half)
+    index[24:32, :] = lag_square(phase_lag, lax.rem(passage + 2 * half - 1 + count, count), 1 - half)
 
 
 def relaxed(current, before, after, weights, forcing, width):
@@ -212,7 +197,7 @@
             target[pl.ds(row, 8), :width] = new
         return carry
 
-    lax.fori_loop(0, 32, tile, 0, unroll=2)
+    lax.fori_loop(0, 32, tile, 0, unroll=True)
     if strips_too:
         for start, first, before, after in ((0, 0, 0, 8), (ROWS - 8, 8, ROWS - 16, ROWS - 8)):
             at = slice(start, start + 8)
@@ -248,7 +233,7 @@
 
 def edges_body(
     first, last, u_l, u_r, w_l, w_r, f_l, f_r, lagged, maps, from_mid, from_plane, phase_lag, to_left, to_right,
-    array, own, other, wide,
+    own, other, index, gaps, array, wide,
 ):
     passage, half = place()
     full = slice(0, W)
@@ -261,8 +246,12 @@
     array[TOP : TOP + 8, :] = jnp.zeros((8, W), F32)
     keep_lagged(own, lagged.at[0])
     keep_lagged(other, from_plane.at[48:56])
-    index = (square(maps[...]), square(from_plane[56:57, :]))
-    fill_gaps(array, own, other, index, lag_pair(phase_lag, passage, half), half, 0)
+    own[8:16] = jnp.zeros((8, 8, 128), F32)
+    other[8:16] = jnp.zeros((8, 8, 128), F32)
+    set_index(index, maps[...], from_plane[56:57, :], phase_lag, passage, half)
+    fill_gaps(array, own, other, index, half, 0)
+    gaps[0:8, :] = array[8:16, :]
+    gaps[8:16, :] = array[TOP : TOP + 8, :]
 
     for out, block, u, w, f, sign in ((to_left, 0, u_l, w_l, f_l, 1), (to_right, 7, u_r, w_r, f_r, -1)):
         lanes = slice(128 * block, 128 * (block + 1))
@@ -287,11 +276,11 @@
     def spec(shape, *at):
         return pl.BlockSpec(shape, lambda i: at)
 
-    whole = [spec((1, 8, W), 0, 0, 0), spec((1, W), 0, 0), spec((48, W), 0, 0), spec((64, W), 0, 0), smem()]
+    whole = [spec((1, 8, W), 0, 0, 0), spec((1, W), 0, 0), spec((48, W), 0, 0), spec((64, W), 0, 0), spec((32, 2), 0, 0)]
     return pl.pallas_call(
         edges_body,
         grid=(1,),
-        out_shape=(EDGE,) * 2,
+        out_shape=(EDGE, EDGE, HISTORY, HISTORY, INDEX, GAPS),
         in_specs=[
             spec((8, W), 0, 0),
             spec((8, W), 31, 0),
@@ -303,10 +292,11 @@
             spec((256, E), 0, 7),
             *whole,
         ],
-        out_specs=(spec((PACKED, E), 0, 0),) * 2,
-        scratch_shapes=[
-            pltpu.VMEM((ROWS, W), F32), pltpu.VMEM((16, 8, 128), F32), pltpu.VMEM((16, 8, 128), F32), pltpu.VMEM((ROWS, E), F32)
-        ],
+        out_specs=(
+            spec((PACKED, E), 0, 0), spec((PACKED, E), 0, 0), spec((16, 8, 128), 0, 0, 0), spec((16, 8, 128), 0, 0, 0),
+            spec((32, 128), 0, 0), spec((16, W), 0, 0),
+        ),
+        scratch_shapes=[pltpu.VMEM((ROWS, W), F32), pltpu.VMEM((ROWS, E), F32)],
         compiler_params=params(),
         name="edges",
     )(field, field, field, field, weights, weights, forcing, forcing, lagged, maps, from_mid, from_plane, phase_lag)
@@ -317,10 +307,10 @@
     array[:, W:] = jnp.where(lane < 64, right, left)
 
 
-def finish(level, source, between, out, surface, weights, forcing, strip, rim, own, other, index, lags, half, tail):
+def finish(level, source, between, out, surface, weights, forcing, strip, rim, own, other, index, half, tail):
     step(source, between, weights, forcing, strip, rim, WX, True)
     surface[0:1, :] = between[16 + 128 : 17 + 128, :W]
-    fill_gaps(between, own, other, index, lags, half, level + 1)
+    fill_gaps(between, own, other, index, half, level + 1)
     step(between, out, weights, forcing, strip, rim, W, not tail)
     row = 128 if tail else 16 + 128
     surface[1:2, :] = out[row : row + 1, :]
@@ -328,17 +318,17 @@
 
 
 def first_body(
-    field, weights, forcing, lagged, maps, from_mid, from_plane, from_left, from_right, phase_lag,
-    out, to_left, to_right, surface, own, other, strip, rim, index, source, between,
+    field, weights, forcing, gaps, from_mid, from_plane, from_left, from_right, own_in, other_in, index,
+    out, to_left, to_right, surface, own, other, strip, rim, source, between,
 ):
-    passage, half = place()
+    _, half = place()
     full = slice(0, W)
     bottom, top = strip_tiles(from_mid, from_plane, half, 0, full)
     source[0:8, :W] = bottom
     source[ROWS - 8 : ROWS, :W] = top
     source[16:TOP, :W] = field[...]
-    source[8:16, :W] = jnp.zeros((8, W), F32)
-    source[TOP : TOP + 8, :W] = jnp.zeros((8, W), F32)
+    source[8:16, :W] = gaps[0:8, :]
+    source[TOP : TOP + 8, :W] = gaps[8:16, :]
     left_edge, right_edge = unpacked_edge(from_left[...], -1), unpacked_edge(from_right[...], 1)
     set_rim(source, left_edge, right_edge)
     lane = lax.broadcasted_iota(jnp.int32, (ROWS, E), 1)
@@ -349,75 +339,64 @@
         right = pltpu.roll(right_edge, 128 - (2 + i), 1)
         left = pltpu.roll(left_edge, 2 + i, 1)
         rim[i, :, :] = jnp.where(lane == 0, right, jnp.where(lane == 127, left, 0.0))
-    keep_lagged(own, lagged.at[0])
-    keep_lagged(other, from_plane.at[48:56])
-    own[8:16] = jnp.zeros((8, 8, 128), F32)
-    other[8:16] = jnp.zeros((8, 8, 128), F32)
-    index[0:8, :] = square(maps[...])
-    index[8:16, :] = square(from_plane[56:57, :])
-    pair = (index[0:8, :], index[8:16, :])
-    lags = lag_pair(phase_lag, passage, half)
-    fill_gaps(source, own, other, pair, lags, half, 0)
+    own[...] = own_in[...]
+    other[...] = other_in[...]
     out[8:16, :] = jnp.zeros((8, W), F32)
     out[TOP : TOP + 8, :] = jnp.zeros((8, W), F32)
     between[8:16, :] = jnp.zeros((8, WX), F32)
     between[TOP : TOP + 8, :] = jnp.zeros((8, WX), F32)
-    finish(0, source, between, out, surface, weights, forcing, strip, rim, own, other, pair, lags, half, False)
-    fill_gaps(out, own, other, pair, lags, half, 2)
+    finish(0, source, between, out, surface, weights, forcing, strip, rim, own, other, index, half, False)
+    fill_gaps(out, own, other, index, half, 2)
     to_left[...] = packed_edge(out[:, :E], 1)
     to_right[...] = packed_edge(out[:, W - E :], -1)
 
 
 def next_body(
-    level, tail, state, weights, forcing, from_left, from_right, own_in, other_in, strip, rim, index, phase_lag, *rest
+    level, tail, state, weights, forcing, from_left, from_right, own_in, other_in, strip, rim, index, *rest
 ):
     if tail:
         out, surface, own, other, source, between = rest
     else:
         out, to_left, to_right, surface, own, other, source, between = rest
-    passage, half = place()
+    _, half = place()
     own[...] = own_in[...]
     other[...] = other_in[...]
     source[:, :W] = state[...]
     set_rim(source, unpacked_edge(from_left[...], -1), unpacked_edge(from_right[...], 1))
     between[8:16, :] = jnp.zeros((8, WX), F32)
     between[TOP : TOP + 8, :] = jnp.zeros((8, WX), F32)
-    pair = (index[0:8, :], index[8:16, :])
-    lags = lag_pair(phase_lag, passage, half)
-    finish(level, source, between, out, surface, weights, forcing, strip, rim, own, other, pair, lags, half, tail)
+    finish(level, source, between, out, surface, weights, forcing, strip, rim, own, other, index, half, tail)
     if not tail:
         out[8:16, :] = jnp.zeros((8, W), F32)
         out[TOP : TOP + 8, :] = jnp.zeros((8, W), F32)
-        fill_gaps(out, own, other, pair, lags, half, level + 2)
+        fill_gaps(out, own, other, index, half, level + 2)
         to_left[...] = packed_edge(out[:, :E], 1)
         to_right[...] = packed_edge(out[:, W - E :], -1)
 
 
-HISTORY = jax.ShapeDtypeStruct((16, 8, 128), F32)
 STATE = jax.ShapeDtypeStruct((ROWS, W), F32)
 BUFFERS = [pltpu.VMEM((ROWS, WX), F32), pltpu.VMEM((ROWS, WX), F32)]
 COST = pl.CostEstimate(flops=2 * 16 * 330 * 1024, bytes_accessed=8 << 20, transcendentals=0)
 
 
-def first_steps(field, weights, forcing, lagged, maps, from_mid, from_plane, from_left, from_right, phase_lag):
+def first_steps(field, weights, forcing, gaps, from_mid, from_plane, from_left, from_right, own, other, index):
     outs = (
         STATE, EDGE, EDGE, jax.ShapeDtypeStruct((8, W), F32), HISTORY, HISTORY,
         jax.ShapeDtypeStruct((5, 16, W), F32), jax.ShapeDtypeStruct((5, ROWS, E), F32),
-        jax.ShapeDtypeStruct((16, 128), jnp.int32),
     )
     return pl.pallas_call(
         first_body,
         out_shape=outs,
-        in_specs=[vmem()] * 9 + [smem()],
+        in_specs=[vmem()] * 11,
         out_specs=tuple(vmem() for _ in outs),
         scratch_shapes=BUFFERS,
         compiler_params=params(),
         cost_estimate=COST,
         name="steps_first",
-    )(field, weights, forcing, lagged, maps, from_mid, from_plane, from_left, from_right, phase_lag)
-
-
-def next_steps(level, state, weights, forcing, from_left, from_right, own, other, strip, rim, index, phase_lag):
+    )(field, weights, forcing, gaps, from_mid, from_plane, from_left, from_right, own, other, index)
+
+
+def next_steps(level, state, weights, forcing, from_left, from_right, own, other, strip, rim, index):
     tail = level == STEPS - 2
     surface = jax.ShapeDtypeStruct((8, W), F32)
     if tail:
@@ -429,13 +408,13 @@
     return pl.pallas_call(
         functools.partial(next_body, level, tail),
         out_shape=outs,
-        in_specs=[vmem()] * 10 + [smem()],
+        in_specs=[vmem()] * 10,
         out_specs=tuple(vmem() for _ in outs),
         scratch_shapes=scratch,
         compiler_params=params(),
         cost_estimate=COST,
         name=f"steps_{level}",
-    )(state, weights, forcing, from_left, from_right, own, other, strip, rim, index, phase_lag)
+    )(state, weights, forcing, from_left, from_right, own, other, strip, rim, index)
 
 
 def kernels_body(points, radius, angle, axial, stagger, area, press, change, *, scale, passages):
@@ -468,7 +447,7 @@
         change[rows, :] = (both * (1.0 / sound_speed)).astype(jnp.bfloat16)
         return carry
 
-    lax.fori_loop(0, press.shape[0] // 16, tile, 0)
+    lax.fori_loop(0, press.shape[0] // 16, tile, 0, unroll=True)
 
 
 def kernels(points, radius, angle, axial, stagger, area, part, count, scale, passages):
@@ -530,6 +509,23 @@
     )(*presses, *changes, record, *surfaces, group)
 
 
+def placed_body(parts, acoustic, array_signal):
+    for s in range(8):
+        acoustic[32 * s : 32 * (s + 1), :] = parts[s, 0:32, :]
+        array_signal[2 * s : 2 * s + 2, :] = parts[s, 32:34, :]
+
+
+def placed(parts):
+    return pl.pallas_call(
+        placed_body,
+        out_shape=(jax.ShapeDtypeStruct((256, 128), F32), jax.ShapeDtypeStruct((GROUPS, 128), F32)),
+        in_specs=[vmem()],
+        out_specs=(vmem(), vmem()),
+        compiler_params=params(),
+        name="placed",
+    )(parts)
+
+
 def exchanged(pieces, axes):
     return lax.all_to_all(pieces, axes, 0, 0, tiled=True)
 
@@ -563,9 +559,10 @@
     rightward = [(i, (i + 1) % cells) for i in range(cells)]
     leftward = [(j, i) for i, j in rightward]
 
-    far = (flow_state, face_weights, forcing, lagged_planes)
-    to_mid, to_plane = strips(*[pltpu.with_memory_space_constraint(x, pltpu.HBM) for x in far], face_map)
-    points, to_mid, to_plane, far = lax.optimization_barrier((listeners.T, to_mid, to_plane, far[:3]))
+    far = (flow_state, face_weights, forcing, lagged_planes, face_map)
+    to_mid, to_plane = strips(*[pltpu.with_memory_space_constraint(x, pltpu.HBM) for x in far])
+    listeners, to_mid, to_plane, far = lax.optimization_barrier((listeners, to_mid, to_plane, far[:3]))
+    points = listeners.T
     from_mid = lax.ppermute(to_mid, PASS, across)
     from_plane = lax.ppermute(to_plane, PASS, over)
 
@@ -577,21 +574,20 @@
     near = load([pltpu.with_memory_space_constraint(x, pltpu.HBM) for x in far])
     pairs, near, from_mid, from_plane = lax.optimization_barrier((pairs, near, from_mid, from_plane))
     flow_state, face_weights, forcing = [pltpu.with_memory_space_constraint(x, pltpu.VMEM) for x in near]
-    to_left, to_right = edges(
+    to_left, to_right, own, other, index, gaps = edges(
         flow_state, face_weights, forcing, lagged_planes, face_map, from_mid, from_plane, phase_lag
     )
     from_left = lax.ppermute(to_right, "cell", rightward)
     from_right = lax.ppermute(to_left, "cell", leftward)
-    state, to_left, to_right, surface, own, other, strip, rim, index = first_steps(
-        flow_state, face_weights, forcing, lagged_planes, face_map, from_mid, from_plane, from_left, from_right,
-        phase_lag,
+    state, to_left, to_right, surface, own, other, strip, rim = first_steps(
+        flow_state, face_weights, forcing, gaps, from_mid, from_plane, from_left, from_right, own, other, index
     )
     surfaces = [surface]
     for level in range(2, STEPS, 2):
         from_left = lax.ppermute(to_right, "cell", rightward)
         from_right = lax.ppermute(to_left, "cell", leftward)
         got = next_steps(
-            level, state, face_weights, forcing, from_left, from_right, own, other, strip, rim, index, phase_lag
+            level, state, face_weights, forcing, from_left, from_right, own, other, strip, rim, index
         )
         if level < STEPS - 2:
             state, to_left, to_right, surface, own, other = got
@@ -604,9 +600,7 @@
     )
     part = jnp.sum(exchanged(pieces, ("x", "y_hi", "cell")), axis=0)
     part = jnp.sum(sent_to_all(part, "z"), axis=0)
-    parts = sent_to_all(part, ("x", "y_hi"))
-    acoustic = parts[:, :32].reshape(256, 128)
-    array_signal = parts[:, 32:34].reshape(GROUPS, 128)
+    acoustic, array_signal = placed(sent_to_all(part, ("x", "y_hi")))
     return state, acoustic, array_signal
 
 

time: 108 us -> 92.4 us (0.86)
  Pallas kernels: 37.3 us -> 19.4 us
  waiting for transfers between devices: 5.62 us -> 9.69 us
  local copies, waits for them, and re-layouts: 3.04 us -> 0.39 us
    pallas_call x3, Pallas kernels: 16.4 us -> 6.97 us  [next_steps(): pl.pallas_call(functools.partial(next_body, level, tail), out_shape=outs,...]
    pallas_call x4, Pallas kernels: 8.01 us -> 3.14 us  [kernels(): pl.pallas_call(functools.partial(kernels_body, scale=scale, passages=pass...]
    ppermute x1, waiting for transfers between devices: 0.01 us -> 4.06 us  [on_device(): from_mid = lax.ppermute(to_mid, PASS, across)]
    pallas_call x2 -> x3, Pallas kernels: 7.48 us -> 3.86 us  [the longest x1 2.54 us: first_steps(): pl.pallas_call(first_body, out_shape=outs, in_specs=[vmem()] * 11, out_sp...]
    unnamed x24 -> x23, local copies, waits for them, and re-layouts: 1.75 us -> 0.15 us
    slice x2 -> x0, local copies, waits for them, and re-layouts: 1.26 us -> none  [the longest x1 0.66 us: on_device(): acoustic = parts[:, :32].reshape(256, 128)]
  transfers between devices with their start and end apart: 10 -> 10, of which waited for: 7 -> 8; matrix products, arithmetic and copies ran while one was open for 0% -> 0% of each run, Pallas kernels for 10% -> 7%
where the time goes in v2:
time: 92.4 us; the launch traced here: 91.4 us
  blocking collectives  44.8 us (48%)
  Pallas kernels  19.4 us (21%)
  starting transfers between devices  16.2 us (18%)
  waiting for transfers between devices  9.69 us (10%)
    all_to_all x3, blocking collectives, exchanged(): return lax.all_to_all(pieces, axes, 0, 0, tiled=True)  44.8 us
    ppermute x1, starting transfers between devices, on_device(): from_plane = lax.ppermute(to_plane, PASS, over)  8.54 us
    pallas_call x3, Pallas kernels, next_steps(): pl.pallas_call(functools.partial(next_body, level, tail), out_shape=outs,...  6.97 us
    ppermute x4, waiting for transfers between devices, on_device(): from_left = lax.ppermute(to_right, 'cell', rightward)  5.13 us
    ppermute x4, starting transfers between devices, on_device(): from_right = lax.ppermute(to_left, 'cell', leftward)  5.04 us
    ppermute x1, waiting for transfers between devices, on_device(): from_mid = lax.ppermute(to_mid, PASS, across)  4.06 us
    pallas_call x4, Pallas kernels, kernels(): pl.pallas_call(functools.partial(kernels_body, scale=scale, passages=pass...  3.14 us
    pallas_call x1, Pallas kernels, load(): pl.pallas_call(load_body, out_shape=tuple((jax.ShapeDtypeStruct(a.shape,...  2.83 us
  transfers between devices with their start and end apart: 10, of which 8 were waited for; matrix products, arithmetic and copies ran while one was open for 0% of the time, Pallas kernels for 7%

profile of v2, /device:TPU:2, one launch (start us, length us, event | category | flops | bytes accessed | tf_op | source)
XLA Modules:
  0.0 91.4 jit_solution(882193907684901980)
XLA Ops:
  0.6 0.0 copy-start.9
  0.6 0.0 copy-start.10
  0.7 1.1 %strips.1 = (f32[48,1024]{1,0:T(8,128)S(1)}, f32[64,1024]{1,0:T(8,128)S(1)}) custom-call(f32[256,1024]{1,0:T(8,128)} %refs_0_, f32[4,256,1024]{2,1,0:T(8,128)} %refs_1_, f32[256,1024]{1,0:T(8,128)} %refs_2_, f32[1,8,1024]{2,1,0:T(8,128)} %lagged.3, s32[1,1024]{1,0:T(1,128)} %maps.3), custom_call_target="tpu_custom_call" | custom-call | tf_op jit(solution)/shard_map/strips/pallas_call | solution.py:71
  1.8 8.5 %collective-permute-start.1 = (f32[64,1024]{1,0:T(8,128)S(1)}, f32[64,1024]{1,0:T(8,128)S(1)}, u32[]{:S(2)}, u32[]{:S(2)}) collective-permute-start(f32[64,1024]{1,0:T(8,128)S(1)} %get-tuple-element.83), channel_id=1, source_target_pairs={{0,252},{4,8},{8,4},{12,16},{16,12},{20,24},{24,20},{28,32},{32,28... | collective-permute-start | bytes 786440 | tf_op jit(solution)/shard_map/ppermute | solution.py:567
  10.3 0.0 collective-permute-start
  10.3 0.1 copy.20.phase_lag
  10.4 0.2 copy.19
  10.6 0.0 copy-start.2
  10.6 0.0 copy-start.3
  10.7 0.0 copy-start.4
  10.7 0.0 copy-start.5
  10.7 0.0 copy-start.6
  10.7 2.8 %load.1 = (f32[256,1024]{1,0:T(8,128)S(1)}, f32[4,256,1024]{2,1,0:T(8,128)S(1)}, f32[256,1024]{1,0:T(8,128)S(1)}) custom-call(f32[256,1024]{1,0:T(8,128)} %refs_0_, f32[4,256,1024]{2,1,0:T(8,128)} %refs_1_, f32[256,1024]{1,0:T(8,128)} %refs_2_), custom_call_target="tpu_custom_call" | custom-call | bytes 12582912 | tf_op jit(solution)/shard_map/load/pallas_call | solution.py:93
  13.5 0.0 copy-start.1
  13.5 0.0 copy-start.7
  13.6 0.8 kernels_3.1
  14.4 0.8 kernels_2.1
  15.2 0.8 kernels_1.1
  16.0 0.8 kernels_0.1
  16.8 4.1 %collective-permute-done.from_mid = f32[48,1024]{1,0:T(8,128)S(1)} collective-permute-done((f32[48,1024]{1,0:T(8,128)S(1)}, f32[48,1024]{1,0:T(8,128)S(1)}, u32[]{:S(2)}, u32[]{:S(2)}) %collective-permute-start) | collective-permute-done | bytes 196640 | tf_op jit(solution)/shard_map/ppermute | solution.py:566
  20.8 0.0 collective-permute-done.1.from_plane
  20.8 0.7 edges.1
  21.5 0.1 collective-permute-start.2
  21.6 1.7 %collective-permute-start.3 = (f32[24,128]{1,0:T(8,128)S(1)}, f32[24,128]{1,0:T(8,128)S(1)}, u32[]{:S(2)}, u32[]{:S(2)}) collective-permute-start(f32[24,128]{1,0:T(8,128)S(1)} %get-tuple-element.91), channel_id=1, source_target_pairs={{1,0},{2,1},{3,2},{0,3},{5,4},{6,5},{7,6},{4,7},{9,8},{10,9},{11,1... | collective-permute-start | bytes 36872 | tf_op jit(solution)/shard_map/ppermute | solution.py:581
  23.3 1.4 %collective-permute-done.2.from_left = f32[24,128]{1,0:T(8,128)S(1)} collective-permute-done((f32[24,128]{1,0:T(8,128)S(1)}, f32[24,128]{1,0:T(8,128)S(1)}, u32[]{:S(2)}, u32[]{:S(2)}) %collective-permute-start.2) | collective-permute-done | bytes 12320 | tf_op jit(solution)/shard_map/ppermute | solution.py:580
  24.7 0.0 collective-permute-done.3.from_right
  24.7 2.5 %steps_first.1 = (f32[288,1024]{1,0:T(8,128)S(1)}, f32[24,128]{1,0:T(8,128)S(1)}, f32[24,128]{1,0:T(8,128)S(1)}, f32[8,1024]{1,0:T(8,128)S(1)}, f32[16,8,128]{2,...) custom-call(f32[256,1024]{1,0:T(8,128)S(1)} %get-tuple-element.84.first.last.u_l, ...), custom_call_target="tpu_custom_call" | custom-call | flops 10813440 | bytes 8388608 | tf_op jit(solution)/shard_map/steps_first/pallas_call | solution.py:387
  27.3 0.8 collective-permute-start.4
  28.1 1.2 %collective-permute-start.5 = (f32[24,128]{1,0:T(8,128)S(1)}, f32[24,128]{1,0:T(8,128)S(1)}, u32[]{:S(2)}, u32[]{:S(2)}) collective-permute-start(f32[24,128]{1,0:T(8,128)S(1)} %get-tuple-element.97), channel_id=1, source_target_pairs={{1,0},{2,1},{3,2},{0,3},{5,4},{6,5},{7,6},{4,7},{9,8},{10,9},{11,1... | collective-permute-start | bytes 36872 | tf_op jit(solution)/shard_map/ppermute | solution.py:588
  29.3 1.1 %collective-permute-done.4.from_left = f32[24,128]{1,0:T(8,128)S(1)} collective-permute-done((f32[24,128]{1,0:T(8,128)S(1)}, f32[24,128]{1,0:T(8,128)S(1)}, u32[]{:S(2)}, u32[]{:S(2)}) %collective-permute-start.4) | collective-permute-done | bytes 12320 | tf_op jit(solution)/shard_map/ppermute | solution.py:587
  30.5 0.3 collective-permute-done.5.from_right
  30.7 2.1 %steps_2.1 = (f32[288,1024]{1,0:T(8,128)S(1)}, f32[24,128]{1,0:T(8,128)S(1)}, f32[24,128]{1,0:T(8,128)S(1)}, f32[8,1024]{1,0:T(8,128)S(1)}, f32[16,8,128]{2,1,0:T(8,128)S(1)}, /*index=5*/f32[16,8,128]{2,1,0:T(8,128)S(1)}) custom-call(f32[288,1024]{1,0:T(8,128)S(1)} %get-tuple-element.95.state, f32[4,256,1024]{2,1,0:T(8,128)S(1)} %get-tuple-element.85.w_l.w_r.weights, ...), custom_call_target="tpu_custom_call" | custom-call | flops 10813440 | bytes 8388608 | tf_op jit(solution)/shard_map/steps_2/pallas_call | solution.py:408
  32.8 0.8 collective-permute-start.6
  33.6 1.0 %collective-permute-start.7 = (f32[24,128]{1,0:T(8,128)S(1)}, f32[24,128]{1,0:T(8,128)S(1)}, u32[]{:S(2)}, u32[]{:S(2)}) collective-permute-start(f32[24,128]{1,0:T(8,128)S(1)} %get-tuple-element.104), channel_id=1, source_target_pairs={{1,0},{2,1},{3,2},{0,3},{5,4},{6,5},{7,6},{4,7},{9,8},{10,9},{11,1... | collective-permute-start | bytes 36872 | tf_op jit(solution)/shard_map/ppermute | solution.py:588
  34.7 1.3 %collective-permute-done.6.from_left = f32[24,128]{1,0:T(8,128)S(1)} collective-permute-done((f32[24,128]{1,0:T(8,128)S(1)}, f32[24,128]{1,0:T(8,128)S(1)}, u32[]{:S(2)}, u32[]{:S(2)}) %collective-permute-start.6) | collective-permute-done | bytes 12320 | tf_op jit(solution)/shard_map/ppermute | solution.py:587
  36.0 0.1 collective-permute-done.7.from_right
  36.1 2.1 %steps_4.1 = (f32[288,1024]{1,0:T(8,128)S(1)}, f32[24,128]{1,0:T(8,128)S(1)}, f32[24,128]{1,0:T(8,128)S(1)}, f32[8,1024]{1,0:T(8,128)S(1)}, f32[16,8,128]{2,1,0:T(8,128)S(1)}, /*index=5*/f32[16,8,128]{2,1,0:T(8,128)S(1)}) custom-call(f32[288,1024]{1,0:T(8,128)S(1)} %get-tuple-element.102.state, f32[4,256,1024]{2,1,0:T(8,128)S(1)} %get-tuple-element.85.w_l.w_r.weights, ...), custom_call_target="tpu_custom_call" | custom-call | flops 10813440 | bytes 8388608 | tf_op jit(solution)/shard_map/steps_4/pallas_call | solution.py:408
  38.2 0.8 collective-permute-start.8
  39.0 1.0 %collective-permute-start.9 = (f32[24,128]{1,0:T(8,128)S(1)}, f32[24,128]{1,0:T(8,128)S(1)}, u32[]{:S(2)}, u32[]{:S(2)}) collective-permute-start(f32[24,128]{1,0:T(8,128)S(1)} %get-tuple-element.109), channel_id=1, source_target_pairs={{1,0},{2,1},{3,2},{0,3},{5,4},{6,5},{7,6},{4,7},{9,8},{10,9},{11,1... | collective-permute-start | bytes 36872 | tf_op jit(solution)/shard_map/ppermute | solution.py:588
  40.0 1.3 %collective-permute-done.8.from_left = f32[24,128]{1,0:T(8,128)S(1)} collective-permute-done((f32[24,128]{1,0:T(8,128)S(1)}, f32[24,128]{1,0:T(8,128)S(1)}, u32[]{:S(2)}, u32[]{:S(2)}) %collective-permute-start.8) | collective-permute-done | bytes 12320 | tf_op jit(solution)/shard_map/ppermute | solution.py:587
  41.4 0.1 collective-permute-done.9.from_right
  41.5 2.8 %steps_6.1 = (f32[256,1024]{1,0:T(8,128)}, f32[8,1024]{1,0:T(8,128)S(1)}) custom-call(f32[288,1024]{1,0:T(8,128)S(1)} %get-tuple-element.107.state, f32[4,256,1024]{2,1,0:T(8,128)S(1)} %get-tuple-element.85.w_l.w_r.weights, f32[256,1024]{1,0:T(8,128)S(1)} %get-tuple-element.86.f_l.f_r.forcing, f32[24,128]{1,0:T(8,128)S(1)} %collective-permute-done.8.from_left, ...), custom_call_target="tpu_custom_call" | custom-call | flops 10813440 | bytes 8388608 | tf_op jit(solution)/shard_map/steps_6/pallas_call | solution.py:408
  44.3 1.5 %sound.1 = f32[32,40,128]{2,1,0:T(8,128)S(1)} custom-call(bf16[256,1024]{1,0:T(8,128)(2,1)S(1)} %get-tuple-element.113.refs_0_, bf16[256,1024]{1,0:T(8,128)(2,1)S(1)} %get-tuple-element.114.refs_1_, bf16[256,1024]{1,0:T(8,128)(2,1)S(1)} %get-tuple-element.115.refs_2_, bf16[256,1024]{1,0:T(8,128)(2,1)S(1)} %get-tuple-element.116.refs_3_, ...), custom_call_target="tpu_custom_call" | custom-call | tf_op jit(solution)/shard_map/sound/pallas_call | solution.py:501
  45.8 16.8 %all_to_all.15 = f32[32,40,128]{2,1,0:T(8,128)S(1)} all-to-all(f32[32,40,128]{2,1,0:T(8,128)S(1)} %sound.1), channel_id=1, replica_groups=mesh['x'=4,'z'=8,'y_hi'=2,'cell'=4] {'x','y_hi','cell'}, dimensions={0} | all-to-all | bytes 1310720 | tf_op jit(solution)/shard_map/all_to_all | solution.py:530
  62.6 0.1 reduce_sum.18
  62.6 17.2 %all_to_all.16 = f32[8,40,128]{2,1,0:T(8,128)S(1)} all-to-all(f32[8,40,128]{2,1,0:T(8,128)S(1)} %broadcast_in_dim.10), channel_id=1, replica_groups=mesh['x'=4,'z'=8,'y_hi'=2,'cell'=4] {'z'}, dimensions={0} | all-to-all | bytes 327680 | tf_op jit(solution)/shard_map/all_to_all | solution.py:530
  79.9 10.8 %all_to_all.17.parts = f32[8,40,128]{2,1,0:T(8,128)S(1)} all-to-all(f32[8,40,128]{2,1,0:T(8,128)S(1)} %broadcast_in_dim.11), channel_id=1, replica_groups=mesh['x'=4,'z'=8,'y_hi'=2,'cell'=4] {'x','y_hi'}, dimensions={0} | all-to-all | bytes 327680 | tf_op jit(solution)/shard_map/all_to_all | solution.py:530
  90.7 0.7 placed.1
  (16 shorter events, 0.1 us)
Async XLA Ops:
  0.6 9.8 %copy-start.9 = (f32[3,1024]{1,0:T(4,128)S(1)}, f32[3,1024]{1,0:T(4,128)}, u32[]{:S(2)}) copy-start(f32[3,1024]{1,0:T(4,128)} %param.26) | copy-start | bytes 36868
  0.6 9.7 %copy-start.10 = (s32[32,2]{0,1:T(2,128)S(1)}, s32[32,2]{0,1:T(2,128)}, u32[]{:S(2)}) copy-start(s32[32,2]{0,1:T(2,128)} %param.18) | copy-start | bytes 772
  1.8 19.1 %collective-permute-start.1 = (f32[64,1024]{1,0:T(8,128)S(1)}, f32[64,1024]{1,0:T(8,128)S(1)}, u32[]{:S(2)}, u32[]{:S(2)}) collective-permute-start(f32[64,1024]{1,0:T(8,128)S(1)} %get-tuple-element.83), channel_id=1, source_target_pairs={{0,252},{4,8},{8,4},{12,16},{16,12},{20,24},{24,20},{28,32},{32,28... | collective-permute-start | bytes 786440 | tf_op jit(solution)/shard_map/ppermute | solution.py:567
  10.3 10.5 %collective-permute-start = (f32[48,1024]{1,0:T(8,128)S(1)}, f32[48,1024]{1,0:T(8,128)S(1)}, u32[]{:S(2)}, u32[]{:S(2)}) collective-permute-start(f32[48,1024]{1,0:T(8,128)S(1)} %get-tuple-element.82), channel_id=1, source_target_pairs={{0,4},{4,0},{8,12},{12,8},{16,20},{20,16},{24,28},{28,24},{32,36},... | collective-permute-start | bytes 589832 | tf_op jit(solution)/shard_map/ppermute | solution.py:566
  10.6 2.9 %copy-start.2 = (f32[2,1024]{1,0:T(2,128)S(1)}, f32[2,1024]{1,0:T(2,128)}, u32[]{:S(2)}) copy-start(f32[2,1024]{1,0:T(2,128)} %radius.7) | copy-start | bytes 24580
  10.6 2.9 %copy-start.3 = (f32[2,1024]{1,0:T(2,128)S(1)}, f32[2,1024]{1,0:T(2,128)}, u32[]{:S(2)}) copy-start(f32[2,1024]{1,0:T(2,128)} %angle.7) | copy-start | bytes 24580
  10.7 2.9 %copy-start.4 = (f32[2,1024]{1,0:T(2,128)S(1)}, f32[2,1024]{1,0:T(2,128)}, u32[]{:S(2)}) copy-start(f32[2,1024]{1,0:T(2,128)} %axial.7) | copy-start | bytes 24580
  10.7 2.9 %copy-start.5 = (f32[2,1024]{1,0:T(2,128)S(1)}, f32[2,1024]{1,0:T(2,128)}, u32[]{:S(2)}) copy-start(f32[2,1024]{1,0:T(2,128)} %stagger.7) | copy-start | bytes 24580
  10.7 2.9 %copy-start.6 = (f32[2,1024]{1,0:T(2,128)S(1)}, f32[2,1024]{1,0:T(2,128)}, u32[]{:S(2)}) copy-start(f32[2,1024]{1,0:T(2,128)} %area.7) | copy-start | bytes 24580
  13.5 7.3 %copy-start.1 = (f32[1,8,1024]{2,1,0:T(8,128)S(1)}, f32[1,8,1024]{2,1,0:T(8,128)}, u32[]{:S(2)}) copy-start(f32[1,8,1024]{2,1,0:T(8,128)} %lagged.3) | copy-start | bytes 98308
  13.5 7.3 %copy-start.7 = (s32[1,1024]{1,0:T(1,128)S(1)}, s32[1,1024]{1,0:T(1,128)}, u32[]{:S(2)}) copy-start(s32[1,1024]{1,0:T(1,128)} %maps.3) | copy-start | bytes 12292
  21.5 3.2 %collective-permute-start.2 = (f32[24,128]{1,0:T(8,128)S(1)}, f32[24,128]{1,0:T(8,128)S(1)}, u32[]{:S(2)}, u32[]{:S(2)}) collective-permute-start(f32[24,128]{1,0:T(8,128)S(1)} %get-tuple-element.90), channel_id=1, source_target_pairs={{0,1},{1,2},{2,3},{3,0},{4,5},{5,6},{6,7},{7,4},{8,9},{9,10},{10,1... | collective-permute-start | bytes 36872 | tf_op jit(solution)/shard_map/ppermute | solution.py:580
  21.6 3.1 %collective-permute-start.3 = (f32[24,128]{1,0:T(8,128)S(1)}, f32[24,128]{1,0:T(8,128)S(1)}, u32[]{:S(2)}, u32[]{:S(2)}) collective-permute-start(f32[24,128]{1,0:T(8,128)S(1)} %get-tuple-element.91), channel_id=1, source_target_pairs={{1,0},{2,1},{3,2},{0,3},{5,4},{6,5},{7,6},{4,7},{9,8},{10,9},{11,1... | collective-permute-start | bytes 36872 | tf_op jit(solution)/shard_map/ppermute | solution.py:581
  27.3 3.2 %collective-permute-start.4 = (f32[24,128]{1,0:T(8,128)S(1)}, f32[24,128]{1,0:T(8,128)S(1)}, u32[]{:S(2)}, u32[]{:S(2)}) collective-permute-start(f32[24,128]{1,0:T(8,128)S(1)} %get-tuple-element.96), channel_id=1, source_target_pairs={{0,1},{1,2},{2,3},{3,0},{4,5},{5,6},{6,7},{7,4},{8,9},{9,10},{10,1... | collective-permute-start | bytes 36872 | tf_op jit(solution)/shard_map/ppermute | solution.py:587
  28.1 2.6 %collective-permute-start.5 = (f32[24,128]{1,0:T(8,128)S(1)}, f32[24,128]{1,0:T(8,128)S(1)}, u32[]{:S(2)}, u32[]{:S(2)}) collective-permute-start(f32[24,128]{1,0:T(8,128)S(1)} %get-tuple-element.97), channel_id=1, source_target_pairs={{1,0},{2,1},{3,2},{0,3},{5,4},{6,5},{7,6},{4,7},{9,8},{10,9},{11,1... | collective-permute-start | bytes 36872 | tf_op jit(solution)/shard_map/ppermute | solution.py:588
  32.8 3.2 %collective-permute-start.6 = (f32[24,128]{1,0:T(8,128)S(1)}, f32[24,128]{1,0:T(8,128)S(1)}, u32[]{:S(2)}, u32[]{:S(2)}) collective-permute-start(f32[24,128]{1,0:T(8,128)S(1)} %get-tuple-element.103), channel_id=1, source_target_pairs={{0,1},{1,2},{2,3},{3,0},{4,5},{5,6},{6,7},{7,4},{8,9},{9,10},{10,1... | collective-permute-start | bytes 36872 | tf_op jit(solution)/shard_map/ppermute | solution.py:587
  33.6 2.4 %collective-permute-start.7 = (f32[24,128]{1,0:T(8,128)S(1)}, f32[24,128]{1,0:T(8,128)S(1)}, u32[]{:S(2)}, u32[]{:S(2)}) collective-permute-start(f32[24,128]{1,0:T(8,128)S(1)} %get-tuple-element.104), channel_id=1, source_target_pairs={{1,0},{2,1},{3,2},{0,3},{5,4},{6,5},{7,6},{4,7},{9,8},{10,9},{11,1... | collective-permute-start | bytes 36872 | tf_op jit(solution)/shard_map/ppermute | solution.py:588
  38.2 3.2 %collective-permute-start.8 = (f32[24,128]{1,0:T(8,128)S(1)}, f32[24,128]{1,0:T(8,128)S(1)}, u32[]{:S(2)}, u32[]{:S(2)}) collective-permute-start(f32[24,128]{1,0:T(8,128)S(1)} %get-tuple-element.108), channel_id=1, source_target_pairs={{0,1},{1,2},{2,3},{3,0},{4,5},{5,6},{6,7},{7,4},{8,9},{9,10},{10,1... | collective-permute-start | bytes 36872 | tf_op jit(solution)/shard_map/ppermute | solution.py:587
  39.0 2.4 %collective-permute-start.9 = (f32[24,128]{1,0:T(8,128)S(1)}, f32[24,128]{1,0:T(8,128)S(1)}, u32[]{:S(2)}, u32[]{:S(2)}) collective-permute-start(f32[24,128]{1,0:T(8,128)S(1)} %get-tuple-element.109), channel_id=1, source_target_pairs={{1,0},{2,1},{3,2},{0,3},{5,4},{6,5},{7,6},{4,7},{9,8},{10,9},{11,1... | collective-permute-start | bytes 36872 | tf_op jit(solution)/shard_map/ppermute | solution.py:588
  41.5 2.8 %copy-start = (bf16[1,120,1024]{2,1,0:T(8,128)(2,1)S(1)}, bf16[1,120,1024]{2,1,0:T(8,128)(2,1)}, u32[]{:S(2)}) copy-start(bf16[1,120,1024]{2,1,0:T(8,128)(2,1)} %refs_8_.1) | copy-start | bytes 737284
  41.5 2.8 %copy-start.8 = (s32[1024]{0:T(1024)S(1)}, s32[1024]{0:T(1024)}, u32[]{:S(2)}) copy-start(s32[1024]{0:T(1024)} %param.27) | copy-start | bytes 12292

commit v3 on v2

--- a/solution.py
+++ b/solution.py
@@ -19,8 +19,9 @@
 TOP = 16 + 256
 ROWS = TOP + 16
 PACKED = 24
-SPLIT = {"x": 4, "z": 8, "y_hi": 2}
+SPLIT = {"x": 4, "z": 8, "y_hi": 2, "y_lo": 2, "core": 2}
 PASS = ("x", "z", "y_hi")
+CELL = ("y_lo", "core")
 VMEM_LIMIT = 8 * 1024 * 1024
 F32 = jnp.float32
 EDGE = jax.ShapeDtypeStruct((PACKED, E), F32)
@@ -63,14 +64,15 @@
         started.append(copy)
     for copy in started:
         copy.wait()
-    to_plane[56:64, :] = jnp.broadcast_to(row[...].astype(F32), (8, W))
+    sub = lax.broadcasted_iota(jnp.int32, (8, W), 0)
+    to_plane[40:48, :] = jnp.where(sub == jnp.where(half == 0, 7, 0), row[...].astype(F32), to_plane[40:48, :])
 
 
 def strips(field, weights, forcing, lagged, maps):
     anywhere = pl.BlockSpec(memory_space=pltpu.HBM)
     return pl.pallas_call(
         strips_body,
-        out_shape=(jax.ShapeDtypeStruct((48, W), F32), jax.ShapeDtypeStruct((64, W), F32)),
+        out_shape=(jax.ShapeDtypeStruct((48, W), F32), jax.ShapeDtypeStruct((56, W), F32)),
         in_specs=[anywhere] * 5,
         out_specs=(vmem(), vmem()),
         scratch_shapes=[pltpu.VMEM((1, W), jnp.int32), pltpu.SemaphoreType.DMA((14,))],
@@ -221,8 +223,8 @@
     for g in range(ROWS // PACKED):
         rows = block[PACKED * g : PACKED * (g + 1)]
         out = jnp.where(spot == g, pltpu.roll(rows, (sign * 8 * g) % E, 1) if g else rows, out)
-    cell = lax.axis_index("cell")
-    end = 0 if sign == 1 else lax.axis_size("cell") - 1
+    cell = lax.axis_index("y_lo") * SPLIT["core"] + lax.axis_index("core")
+    end = 0 if sign == 1 else SPLIT["y_lo"] * SPLIT["core"] - 1
     return jnp.where(cell == end, 0.0, out)
 
 
@@ -248,7 +250,8 @@
     keep_lagged(other, from_plane.at[48:56])
     own[8:16] = jnp.zeros((8, 8, 128), F32)
     other[8:16] = jnp.zeros((8, 8, 128), F32)
-    set_index(index, maps[...], from_plane[56:57, :], phase_lag, passage, half)
+    other_maps = jnp.where(half == 0, from_plane[40:41, :], from_plane[47:48, :])
+    set_index(index, maps[...], other_maps, phase_lag, passage, half)
     fill_gaps(array, own, other, index, half, 0)
     gaps[0:8, :] = array[8:16, :]
     gaps[8:16, :] = array[TOP : TOP + 8, :]
@@ -276,7 +279,7 @@
     def spec(shape, *at):
         return pl.BlockSpec(shape, lambda i: at)
 
-    whole = [spec((1, 8, W), 0, 0, 0), spec((1, W), 0, 0), spec((48, W), 0, 0), spec((64, W), 0, 0), spec((32, 2), 0, 0)]
+    whole = [spec((1, 8, W), 0, 0, 0), spec((1, W), 0, 0), spec((48, W), 0, 0), spec((56, W), 0, 0), spec((32, 2), 0, 0)]
     return pl.pallas_call(
         edges_body,
         grid=(1,),
@@ -467,7 +470,7 @@
 
 
 def sound_body(*refs):
-    presses, changes, (record, s0, s1, s2, s3, group, out, total) = refs[:4], refs[4:8], refs[8:]
+    presses, changes, (record, s0, s1, s2, s3, group, keep, give, total) = refs[:4], refs[4:8], refs[8:]
     late = jnp.concatenate([s[0:2, :] for s in (s0, s1, s2, s3)], axis=0).astype(jnp.bfloat16)
     surface = jnp.concatenate([record[0].astype(F32), late.astype(F32)], axis=0)
     times = surface.shape[0]
@@ -489,20 +492,21 @@
     counts = jnp.sum(member, axis=1, keepdims=True)
     means = jnp.dot(member, total[...], precision=lax.Precision.HIGHEST, preferred_element_type=F32)
     means = means / jnp.maximum(counts, 1.0)
-    for s in range(8):
-        for c in range(4):
-            start = 256 * c + 32 * s
-            out[4 * s + c, 0:32, :] = total[start : start + 32, :]
-            out[4 * s + c, 32:34, :] = means[2 * s : 2 * s + 2, :]
-            out[4 * s + c, 34:40, :] = jnp.zeros((6, 128), F32)
+    core = lax.axis_index("core")
+    for out, to in ((keep, core), (give, 1 - core)):
+        for s in range(8):
+            for c in range(2):
+                start = pl.multiple_of(512 * c + 32 * s + 256 * to, 32)
+                out[2 * s + c, 0:16] = total[pl.ds(start, 32), :].reshape(16, 2, 128)
+                out[2 * s + c, 16] = means[2 * s : 2 * s + 2, :]
 
 
 def sound(presses, changes, record, surfaces, group):
     return pl.pallas_call(
         sound_body,
-        out_shape=jax.ShapeDtypeStruct((32, 40, 128), F32),
+        out_shape=(jax.ShapeDtypeStruct((16, 17, 2, 128), F32),) * 2,
         in_specs=[vmem()] * 14,
-        out_specs=vmem(),
+        out_specs=(vmem(), vmem()),
         scratch_shapes=[pltpu.VMEM((1024, 128), F32)],
         compiler_params=params(),
         name="sound",
@@ -511,8 +515,8 @@
 
 def placed_body(parts, acoustic, array_signal):
     for s in range(8):
-        acoustic[32 * s : 32 * (s + 1), :] = parts[s, 0:32, :]
-        array_signal[2 * s : 2 * s + 2, :] = parts[s, 32:34, :]
+        acoustic[32 * s : 32 * (s + 1), :] = parts[s, 0:16].reshape(32, 128)
+        array_signal[2 * s : 2 * s + 2, :] = parts[s, 16]
 
 
 def placed(parts):
@@ -524,6 +528,40 @@
         compiler_params=params(),
         name="placed",
     )(parts)
+
+
+def store_body(state, after, out, sem):
+    copy = pltpu.make_async_copy(state, out, sem)
+    copy.start()
+    copy.wait()
+
+
+def store(state, after):
+    return pl.pallas_call(
+        store_body,
+        out_shape=jax.ShapeDtypeStruct(state.shape, F32),
+        in_specs=[vmem(), pl.BlockSpec(memory_space=pl.ANY)],
+        out_specs=pl.BlockSpec(memory_space=pltpu.HBM),
+        scratch_shapes=[pltpu.SemaphoreType.DMA],
+        compiler_params=params(),
+        cost_estimate=pl.CostEstimate(flops=0, bytes_accessed=2 << 20, transcendentals=0),
+        name="store",
+    )(pltpu.with_memory_space_constraint(state, pltpu.VMEM), after)
+
+
+def merged_body(keep, got, after, out):
+    out[...] = keep[...] + got[...]
+
+
+def merged(keep, got, after):
+    return pl.pallas_call(
+        merged_body,
+        out_shape=jax.ShapeDtypeStruct(keep.shape, F32),
+        in_specs=[vmem(), vmem(), pl.BlockSpec(memory_space=pl.ANY)],
+        out_specs=vmem(),
+        compiler_params=params(),
+        name="merged",
+    )(keep, got, after)
 
 
 def exchanged(pieces, axes):
@@ -552,7 +590,7 @@
     observer_group,
 ):
     passes = lax.axis_size(PASS)
-    cells = lax.axis_size("cell")
+    cells = lax.axis_size(CELL)
     scale = 64.0 / math.sqrt(W * cells * passes)
     across = [(i, i ^ 1) for i in range(passes)]
     over = [(i, ((i + 1) ^ 1) - 1 if 0 < i < passes - 1 else passes - 1 - i) for i in range(passes)]
@@ -577,15 +615,15 @@
     to_left, to_right, own, other, index, gaps = edges(
         flow_state, face_weights, forcing, lagged_planes, face_map, from_mid, from_plane, phase_lag
     )
-    from_left = lax.ppermute(to_right, "cell", rightward)
-    from_right = lax.ppermute(to_left, "cell", leftward)
+    from_left = lax.ppermute(to_right, CELL, rightward)
+    from_right = lax.ppermute(to_left, CELL, leftward)
     state, to_left, to_right, surface, own, other, strip, rim = first_steps(
         flow_state, face_weights, forcing, gaps, from_mid, from_plane, from_left, from_right, own, other, index
     )
     surfaces = [surface]
     for level in range(2, STEPS, 2):
-        from_left = lax.ppermute(to_right, "cell", rightward)
-        from_right = lax.ppermute(to_left, "cell", leftward)
+        from_left = lax.ppermute(to_right, CELL, rightward)
+        from_right = lax.ppermute(to_left, CELL, leftward)
         got = next_steps(
             level, state, face_weights, forcing, from_left, from_right, own, other, strip, rim, index
         )
@@ -595,37 +633,39 @@
             state, surface = got
         surfaces.append(surface)
 
-    pieces = sound(
+    keep, give = sound(
         [p[0] for p in pairs], [p[1] for p in pairs], surface_record, surfaces, observer_group[None, :]
     )
-    part = jnp.sum(exchanged(pieces, ("x", "y_hi", "cell")), axis=0)
+    state = store(state, keep)
+    got = lax.ppermute(give, "core", [(0, 1), (1, 0)])
+    pieces = merged(keep, got, pltpu.with_memory_space_constraint(state, pltpu.HBM))
+    part = jnp.sum(exchanged(pieces, ("x", "y_hi", "y_lo")), axis=0)
     part = jnp.sum(sent_to_all(part, "z"), axis=0)
     acoustic, array_signal = placed(sent_to_all(part, ("x", "y_hi")))
     return state, acoustic, array_signal
 
 
 def solution(mesh):
-    sizes = tuple(SPLIT.values())
-    fine = Mesh(mesh.devices.reshape(*sizes, mesh.shape["cell"]), (*PASS, "cell"))
+    fine = Mesh(mesh.devices.reshape(*SPLIT.values()), tuple(SPLIT))
     return jax.shard_map(
         on_device,
         mesh=fine,
         in_specs=(
-            P(PASS, "cell"),
-            P(None, PASS, "cell"),
-            P(PASS, "cell"),
-            P(PASS, None, "cell"),
+            P(PASS, CELL),
+            P(None, PASS, CELL),
+            P(PASS, CELL),
+            P(PASS, None, CELL),
             P(),
-            P(PASS, "cell"),
-            P(PASS, None, "cell"),
-            P(None, "cell"),
-            P(None, "cell"),
-            P(None, "cell"),
-            P(None, "cell"),
-            P(None, "cell"),
+            P(PASS, CELL),
+            P(PASS, None, CELL),
+            P(None, CELL),
+            P(None, CELL),
+            P(None, CELL),
+            P(None, CELL),
+            P(None, CELL),
             P(),
             P(),
         ),
-        out_specs=(P(PASS, "cell"), P("cell", None), P()),
+        out_specs=(P(PASS, CELL), P(CELL, None), P()),
         check_vma=False,
     )

time: 92.4 us -> 87.8 us (0.950)
  blocking collectives: 44.8 us -> 40 us
    all_to_all x3, blocking collectives: 44.8 us -> 40 us  [exchanged(): return lax.all_to_all(pieces, axes, 0, 0, tiled=True)]
    pallas_call x1 -> x3, Pallas kernels: 1.49 us -> 2.86 us  [the longest x1 1.74 us: sound(): pl.pallas_call(sound_body, out_shape=(jax.ShapeDtypeStruct((16, 17, 2, 12...]
    pallas_call x3, Pallas kernels: 6.97 us -> 5.98 us  [next_steps(): pl.pallas_call(functools.partial(next_body, level, tail), out_shape=outs,...]
    ppermute x8 -> x9, starting transfers between devices: 7.65 us -> 8.5 us  [the longest x4 5.04 us: on_device(): from_right = lax.ppermute(to_left, CELL, leftward)]
    ppermute x8 -> x9, waiting for transfers between devices: 5.62 us -> 5.82 us  [the longest x4 5.13 us: on_device(): from_left = lax.ppermute(to_right, CELL, rightward)]
  transfers between devices with their start and end apart: 10 -> 11, of which waited for: 8 -> 9; matrix products, arithmetic and copies ran while one was open for 0% -> 0% of each run, Pallas kernels for 7% -> 8%
where the time goes in v3:
time: 87.8 us; the launch traced here: 87.5 us
  blocking collectives  40 us (46%)
  Pallas kernels  19.8 us (23%)
  starting transfers between devices  17 us (19%)
  waiting for transfers between devices  9.18 us (10%)
    all_to_all x3, blocking collectives, exchanged(): return lax.all_to_all(pieces, axes, 0, 0, tiled=True)  40 us
    ppermute x1, starting transfers between devices, on_device(): from_plane = lax.ppermute(to_plane, PASS, over)  8.54 us
    pallas_call x3, Pallas kernels, next_steps(): pl.pallas_call(functools.partial(next_body, level, tail), out_shape=outs,...  5.98 us
    ppermute x4, waiting for transfers between devices, on_device(): from_left = lax.ppermute(to_right, CELL, rightward)  5.13 us
    ppermute x4, starting transfers between devices, on_device(): from_right = lax.ppermute(to_left, CELL, leftward)  5.04 us
    ppermute x1, waiting for transfers between devices, on_device(): from_mid = lax.ppermute(to_mid, PASS, across)  3.36 us
    pallas_call x4, Pallas kernels, kernels(): pl.pallas_call(functools.partial(kernels_body, scale=scale, passages=pass...  3.14 us
    pallas_call x1, Pallas kernels, load(): pl.pallas_call(load_body, out_shape=tuple((jax.ShapeDtypeStruct(a.shape,...  2.83 us
  transfers between devices with their start and end apart: 11, of which 9 were waited for; matrix products, arithmetic and copies ran while one was open for 0% of the time, Pallas kernels for 8%

profile of v3, /device:TPU:2, one launch (start us, length us, event | category | flops | bytes accessed | tf_op | source)
XLA Modules:
  0.0 87.5 jit_solution(18222351990164548076)
XLA Ops:
  0.7 1.1 %strips.1 = (f32[48,1024]{1,0:T(8,128)S(1)}, f32[56,1024]{1,0:T(8,128)S(1)}) custom-call(f32[256,1024]{1,0:T(8,128)} %refs_0_, f32[4,256,1024]{2,1,0:T(8,128)} %refs_1_, f32[256,1024]{1,0:T(8,128)} %refs_2_, f32[1,8,1024]{2,1,0:T(8,128)} %lagged.3, s32[1,1024]{1,0:T(1,128)} %maps.3), custom_call_target="tpu_custom_call" | custom-call | tf_op jit(solution)/shard_map/strips/pallas_call | solution.py:73
  1.8 8.5 %collective-permute-start.1 = (f32[56,1024]{1,0:T(8,128)S(1)}, f32[56,1024]{1,0:T(8,128)S(1)}, u32[]{:S(2)}, u32[]{:S(2)}) collective-permute-start(f32[56,1024]{1,0:T(8,128)S(1)} %get-tuple-element.85), channel_id=1, source_target_pairs={{0,252},{4,8},{8,4},{12,16},{16,12},{20,24},{24,20},{28,32},{32,28... | collective-permute-start | bytes 688136 | tf_op jit(solution)/shard_map/ppermute | solution.py:605
  10.3 0.1 copy.22.phase_lag
  10.4 0.2 copy.21
  10.6 0.0 copy-start.2
  10.6 0.0 copy-start.3
  10.7 0.0 copy-start.4
  10.7 0.0 copy-start.5
  10.7 0.0 copy-start.6
  10.7 2.8 %load.1 = (f32[256,1024]{1,0:T(8,128)S(1)}, f32[4,256,1024]{2,1,0:T(8,128)S(1)}, f32[256,1024]{1,0:T(8,128)S(1)}) custom-call(f32[256,1024]{1,0:T(8,128)} %refs_0_, f32[4,256,1024]{2,1,0:T(8,128)} %refs_1_, f32[256,1024]{1,0:T(8,128)} %refs_2_), custom_call_target="tpu_custom_call" | custom-call | bytes 12582912 | tf_op jit(solution)/shard_map/load/pallas_call | solution.py:95
  13.5 0.0 copy-start.1
  13.6 0.8 kernels_3.1
  14.4 0.8 kernels_2.1
  15.2 0.8 kernels_1.1
  16.0 0.8 kernels_0.1
  16.8 3.4 %collective-permute-done.from_mid = f32[48,1024]{1,0:T(8,128)S(1)} collective-permute-done((f32[48,1024]{1,0:T(8,128)S(1)}, f32[48,1024]{1,0:T(8,128)S(1)}, u32[]{:S(2)}, u32[]{:S(2)}) %collective-permute-start) | collective-permute-done | bytes 196640 | tf_op jit(solution)/shard_map/ppermute | solution.py:604
  20.1 0.7 edges.1
  20.8 0.1 collective-permute-start.2
  20.9 1.7 %collective-permute-start.3 = (f32[24,128]{1,0:T(8,128)S(1)}, f32[24,128]{1,0:T(8,128)S(1)}, u32[]{:S(2)}, u32[]{:S(2)}) collective-permute-start(f32[24,128]{1,0:T(8,128)S(1)} %get-tuple-element.93), channel_id=1, source_target_pairs={{1,0},{2,1},{3,2},{0,3},{5,4},{6,5},{7,6},{4,7},{9,8},{10,9},{11,1... | collective-permute-start | bytes 36872 | tf_op jit(solution)/shard_map/ppermute | solution.py:619
  22.6 1.4 %collective-permute-done.2.from_left = f32[24,128]{1,0:T(8,128)S(1)} collective-permute-done((f32[24,128]{1,0:T(8,128)S(1)}, f32[24,128]{1,0:T(8,128)S(1)}, u32[]{:S(2)}, u32[]{:S(2)}) %collective-permute-start.2) | collective-permute-done | bytes 12320 | tf_op jit(solution)/shard_map/ppermute | solution.py:618
  24.0 0.0 collective-permute-done.3.from_right
  24.0 2.5 %steps_first.1 = (f32[288,1024]{1,0:T(8,128)S(1)}, f32[24,128]{1,0:T(8,128)S(1)}, f32[24,128]{1,0:T(8,128)S(1)}, f32[8,1024]{1,0:T(8,128)S(1)}, f32[16,8,128]{2,...) custom-call(f32[256,1024]{1,0:T(8,128)S(1)} %get-tuple-element.86.first.last.u_l, ...), custom_call_target="tpu_custom_call" | custom-call | flops 10813440 | bytes 8388608 | tf_op jit(solution)/shard_map/steps_first/pallas_call | solution.py:390
  26.6 0.8 collective-permute-start.4
  27.4 1.2 %collective-permute-start.5 = (f32[24,128]{1,0:T(8,128)S(1)}, f32[24,128]{1,0:T(8,128)S(1)}, u32[]{:S(2)}, u32[]{:S(2)}) collective-permute-start(f32[24,128]{1,0:T(8,128)S(1)} %get-tuple-element.99), channel_id=1, source_target_pairs={{1,0},{2,1},{3,2},{0,3},{5,4},{6,5},{7,6},{4,7},{9,8},{10,9},{11,1... | collective-permute-start | bytes 36872 | tf_op jit(solution)/shard_map/ppermute | solution.py:626
  28.6 1.1 %collective-permute-done.4.from_left = f32[24,128]{1,0:T(8,128)S(1)} collective-permute-done((f32[24,128]{1,0:T(8,128)S(1)}, f32[24,128]{1,0:T(8,128)S(1)}, u32[]{:S(2)}, u32[]{:S(2)}) %collective-permute-start.4) | collective-permute-done | bytes 12320 | tf_op jit(solution)/shard_map/ppermute | solution.py:625
  29.8 0.3 collective-permute-done.5.from_right
  30.0 2.1 %steps_2.1 = (f32[288,1024]{1,0:T(8,128)S(1)}, f32[24,128]{1,0:T(8,128)S(1)}, f32[24,128]{1,0:T(8,128)S(1)}, f32[8,1024]{1,0:T(8,128)S(1)}, f32[16,8,128]{2,1,0:T(8,128)S(1)}, /*index=5*/f32[16,8,128]{2,1,0:T(8,128)S(1)}) custom-call(f32[288,1024]{1,0:T(8,128)S(1)} %get-tuple-element.97.state, f32[4,256,1024]{2,1,0:T(8,128)S(1)} %get-tuple-element.87.w_l.w_r.weights, ...), custom_call_target="tpu_custom_call" | custom-call | flops 10813440 | bytes 8388608 | tf_op jit(solution)/shard_map/steps_2/pallas_call | solution.py:411
  32.1 0.8 collective-permute-start.6
  32.9 1.0 %collective-permute-start.7 = (f32[24,128]{1,0:T(8,128)S(1)}, f32[24,128]{1,0:T(8,128)S(1)}, u32[]{:S(2)}, u32[]{:S(2)}) collective-permute-start(f32[24,128]{1,0:T(8,128)S(1)} %get-tuple-element.106), channel_id=1, source_target_pairs={{1,0},{2,1},{3,2},{0,3},{5,4},{6,5},{7,6},{4,7},{9,8},{10,9},{11,1... | collective-permute-start | bytes 36872 | tf_op jit(solution)/shard_map/ppermute | solution.py:626
  34.0 1.3 %collective-permute-done.6.from_left = f32[24,128]{1,0:T(8,128)S(1)} collective-permute-done((f32[24,128]{1,0:T(8,128)S(1)}, f32[24,128]{1,0:T(8,128)S(1)}, u32[]{:S(2)}, u32[]{:S(2)}) %collective-permute-start.6) | collective-permute-done | bytes 12320 | tf_op jit(solution)/shard_map/ppermute | solution.py:625
  35.3 0.1 collective-permute-done.7.from_right
  35.4 2.1 %steps_4.1 = (f32[288,1024]{1,0:T(8,128)S(1)}, f32[24,128]{1,0:T(8,128)S(1)}, f32[24,128]{1,0:T(8,128)S(1)}, f32[8,1024]{1,0:T(8,128)S(1)}, f32[16,8,128]{2,1,0:T(8,128)S(1)}, /*index=5*/f32[16,8,128]{2,1,0:T(8,128)S(1)}) custom-call(f32[288,1024]{1,0:T(8,128)S(1)} %get-tuple-element.104.state, f32[4,256,1024]{2,1,0:T(8,128)S(1)} %get-tuple-element.87.w_l.w_r.weights, ...), custom_call_target="tpu_custom_call" | custom-call | flops 10813440 | bytes 8388608 | tf_op jit(solution)/shard_map/steps_4/pallas_call | solution.py:411
  37.5 0.8 collective-permute-start.8
  38.3 1.0 %collective-permute-start.9 = (f32[24,128]{1,0:T(8,128)S(1)}, f32[24,128]{1,0:T(8,128)S(1)}, u32[]{:S(2)}, u32[]{:S(2)}) collective-permute-start(f32[24,128]{1,0:T(8,128)S(1)} %get-tuple-element.111), channel_id=1, source_target_pairs={{1,0},{2,1},{3,2},{0,3},{5,4},{6,5},{7,6},{4,7},{9,8},{10,9},{11,1... | collective-permute-start | bytes 36872 | tf_op jit(solution)/shard_map/ppermute | solution.py:626
  39.3 1.3 %collective-permute-done.8.from_left = f32[24,128]{1,0:T(8,128)S(1)} collective-permute-done((f32[24,128]{1,0:T(8,128)S(1)}, f32[24,128]{1,0:T(8,128)S(1)}, u32[]{:S(2)}, u32[]{:S(2)}) %collective-permute-start.8) | collective-permute-done | bytes 12320 | tf_op jit(solution)/shard_map/ppermute | solution.py:625
  40.7 0.1 collective-permute-done.9.from_right
  40.8 1.8 %steps_6.1 = (f32[256,1024]{1,0:T(8,128)S(1)}, f32[8,1024]{1,0:T(8,128)S(1)}) custom-call(f32[288,1024]{1,0:T(8,128)S(1)} %get-tuple-element.109.state, f32[4,256,1024]{2,1,0:T(8,128)S(1)} %get-tuple-element.87.w_l.w_r.weights, f32[256,1024]{1,0:T(8,128)S(1)} %get-tuple-element.88.f_l.f_r.forcing, f32[24,128]{1,0:T(8,128)S(1)} %collective-permute-done.8.from_left, ...), custom_call_target="tpu_custom_call" | custom-call | flops 10813440 | bytes 8388608 | tf_op jit(solution)/shard_map/steps_6/pallas_call | solution.py:411
  42.6 1.7 %sound.1 = (f32[16,17,2,128]{3,2,1,0:T(2,128)S(1)}, f32[16,17,2,128]{3,2,1,0:T(2,128)S(1)}) custom-call(bf16[256,1024]{1,0:T(8,128)(2,1)S(1)} %get-tuple-element.115.refs_0_, bf16[256,1024]{1,0:T(8,128)(2,1)S(1)} %get-tuple-element.116.refs_1_, bf16[256,1024]{1,0:T(8,128)(2,1)S(1)} %get-tuple-element.117.refs_2_, ...), custom_call_target="tpu_custom_call" | custom-call | tf_op jit(solution)/shard_map/sound/pallas_call | solution.py:505
  44.4 0.8 collective-permute-start.10
  45.2 1.0 %store.1.after = f32[256,1024]{1,0:T(8,128)} custom-call(f32[256,1024]{1,0:T(8,128)S(1)} %get-tuple-element.114.state, f32[16,17,2,128]{3,2,1,0:T(2,128)S(1)} %get-tuple-element.127.after.keep), custom_call_target="tpu_custom_call" | custom-call | bytes 2097152 | tf_op jit(solution)/shard_map/store/pallas_call | solution.py:540
  46.2 0.2 collective-permute-done.10.got
  46.4 0.1 merged.1
  46.5 13.0 %all_to_all.15 = f32[16,17,2,128]{3,2,1,0:T(2,128)S(1)} all-to-all(f32[16,17,2,128]{3,2,1,0:T(2,128)S(1)} %merged.1), channel_id=1, replica_groups=mesh['x'=4,'z'=8,'y_hi'=2,'y_lo'=2,'core'=2] {'x','y_hi','y_lo'}, dimensions={0} | all-to-all | bytes 557056 | tf_op jit(solution)/shard_map/all_to_all | solution.py:568
  59.6 0.1 reduce_sum.18
  59.7 15.4 %all_to_all.16 = f32[8,17,2,128]{3,2,1,0:T(2,128)S(1)} all-to-all(f32[8,17,2,128]{3,2,1,0:T(2,128)S(1)} %broadcast_in_dim.10), channel_id=1, replica_groups=mesh['x'=4,'z'=8,'y_hi'=2,'y_lo'=2,'core'=2] {'z'}, dimensions={0} | all-to-all | bytes 278528 | tf_op jit(solution)/shard_map/all_to_all | solution.py:568
  75.2 0.1 reduce_sum.19
  75.2 11.6 %all_to_all.17.parts = f32[8,17,2,128]{3,2,1,0:T(2,128)S(1)} all-to-all(f32[8,17,2,128]{3,2,1,0:T(2,128)S(1)} %broadcast_in_dim.11), channel_id=1, replica_groups=mesh['x'=4,'z'=8,'y_hi'=2,'y_lo'=2,'core'=2] {'x','y_hi'}, dimensions={0} | all-to-all | bytes 278528 | tf_op jit(solution)/shard_map/all_to_all | solution.py:568
  86.8 0.7 placed.1
  (20 shorter events, 0.1 us)
Async XLA Ops:
  0.6 9.8 %copy-start.9 = (f32[3,1024]{1,0:T(4,128)S(1)}, f32[3,1024]{1,0:T(4,128)}, u32[]{:S(2)}) copy-start(f32[3,1024]{1,0:T(4,128)} %param.26) | copy-start | bytes 36868
  0.6 9.7 %copy-start.10 = (s32[32,2]{0,1:T(2,128)S(1)}, s32[32,2]{0,1:T(2,128)}, u32[]{:S(2)}) copy-start(s32[32,2]{0,1:T(2,128)} %param.18) | copy-start | bytes 772
  1.8 18.4 %collective-permute-start.1 = (f32[56,1024]{1,0:T(8,128)S(1)}, f32[56,1024]{1,0:T(8,128)S(1)}, u32[]{:S(2)}, u32[]{:S(2)}) collective-permute-start(f32[56,1024]{1,0:T(8,128)S(1)} %get-tuple-element.85), channel_id=1, source_target_pairs={{0,252},{4,8},{8,4},{12,16},{16,12},{20,24},{24,20},{28,32},{32,28... | collective-permute-start | bytes 688136 | tf_op jit(solution)/shard_map/ppermute | solution.py:605
  10.3 9.8 %collective-permute-start = (f32[48,1024]{1,0:T(8,128)S(1)}, f32[48,1024]{1,0:T(8,128)S(1)}, u32[]{:S(2)}, u32[]{:S(2)}) collective-permute-start(f32[48,1024]{1,0:T(8,128)S(1)} %get-tuple-element.84), channel_id=1, source_target_pairs={{0,4},{4,0},{8,12},{12,8},{16,20},{20,16},{24,28},{28,24},{32,36},... | collective-permute-start | bytes 589832 | tf_op jit(solution)/shard_map/ppermute | solution.py:604
  10.6 2.9 %copy-start.2 = (f32[2,1024]{1,0:T(2,128)S(1)}, f32[2,1024]{1,0:T(2,128)}, u32[]{:S(2)}) copy-start(f32[2,1024]{1,0:T(2,128)} %radius.7) | copy-start | bytes 24580
  10.6 2.9 %copy-start.3 = (f32[2,1024]{1,0:T(2,128)S(1)}, f32[2,1024]{1,0:T(2,128)}, u32[]{:S(2)}) copy-start(f32[2,1024]{1,0:T(2,128)} %angle.7) | copy-start | bytes 24580
  10.7 2.9 %copy-start.4 = (f32[2,1024]{1,0:T(2,128)S(1)}, f32[2,1024]{1,0:T(2,128)}, u32[]{:S(2)}) copy-start(f32[2,1024]{1,0:T(2,128)} %axial.7) | copy-start | bytes 24580
  10.7 2.9 %copy-start.5 = (f32[2,1024]{1,0:T(2,128)S(1)}, f32[2,1024]{1,0:T(2,128)}, u32[]{:S(2)}) copy-start(f32[2,1024]{1,0:T(2,128)} %stagger.7) | copy-start | bytes 24580
  10.7 2.9 %copy-start.6 = (f32[2,1024]{1,0:T(2,128)S(1)}, f32[2,1024]{1,0:T(2,128)}, u32[]{:S(2)}) copy-start(f32[2,1024]{1,0:T(2,128)} %area.7) | copy-start | bytes 24580
  13.5 6.6 %copy-start.1 = (f32[1,8,1024]{2,1,0:T(8,128)S(1)}, f32[1,8,1024]{2,1,0:T(8,128)}, u32[]{:S(2)}) copy-start(f32[1,8,1024]{2,1,0:T(8,128)} %lagged.3) | copy-start | bytes 98308
  13.5 6.6 %copy-start.7 = (s32[1,1024]{1,0:T(1,128)S(1)}, s32[1,1024]{1,0:T(1,128)}, u32[]{:S(2)}) copy-start(s32[1,1024]{1,0:T(1,128)} %maps.3) | copy-start | bytes 12292
  20.8 3.2 %collective-permute-start.2 = (f32[24,128]{1,0:T(8,128)S(1)}, f32[24,128]{1,0:T(8,128)S(1)}, u32[]{:S(2)}, u32[]{:S(2)}) collective-permute-start(f32[24,128]{1,0:T(8,128)S(1)} %get-tuple-element.92), channel_id=1, source_target_pairs={{0,1},{1,2},{2,3},{3,0},{4,5},{5,6},{6,7},{7,4},{8,9},{9,10},{10,1... | collective-permute-start | bytes 36872 | tf_op jit(solution)/shard_map/ppermute | solution.py:618
  20.9 3.1 %collective-permute-start.3 = (f32[24,128]{1,0:T(8,128)S(1)}, f32[24,128]{1,0:T(8,128)S(1)}, u32[]{:S(2)}, u32[]{:S(2)}) collective-permute-start(f32[24,128]{1,0:T(8,128)S(1)} %get-tuple-element.93), channel_id=1, source_target_pairs={{1,0},{2,1},{3,2},{0,3},{5,4},{6,5},{7,6},{4,7},{9,8},{10,9},{11,1... | collective-permute-start | bytes 36872 | tf_op jit(solution)/shard_map/ppermute | solution.py:619
  26.6 3.2 %collective-permute-start.4 = (f32[24,128]{1,0:T(8,128)S(1)}, f32[24,128]{1,0:T(8,128)S(1)}, u32[]{:S(2)}, u32[]{:S(2)}) collective-permute-start(f32[24,128]{1,0:T(8,128)S(1)} %get-tuple-element.98), channel_id=1, source_target_pairs={{0,1},{1,2},{2,3},{3,0},{4,5},{5,6},{6,7},{7,4},{8,9},{9,10},{10,1... | collective-permute-start | bytes 36872 | tf_op jit(solution)/shard_map/ppermute | solution.py:625
  27.4 2.6 %collective-permute-start.5 = (f32[24,128]{1,0:T(8,128)S(1)}, f32[24,128]{1,0:T(8,128)S(1)}, u32[]{:S(2)}, u32[]{:S(2)}) collective-permute-start(f32[24,128]{1,0:T(8,128)S(1)} %get-tuple-element.99), channel_id=1, source_target_pairs={{1,0},{2,1},{3,2},{0,3},{5,4},{6,5},{7,6},{4,7},{9,8},{10,9},{11,1... | collective-permute-start | bytes 36872 | tf_op jit(solution)/shard_map/ppermute | solution.py:626
  32.1 3.2 %collective-permute-start.6 = (f32[24,128]{1,0:T(8,128)S(1)}, f32[24,128]{1,0:T(8,128)S(1)}, u32[]{:S(2)}, u32[]{:S(2)}) collective-permute-start(f32[24,128]{1,0:T(8,128)S(1)} %get-tuple-element.105), channel_id=1, source_target_pairs={{0,1},{1,2},{2,3},{3,0},{4,5},{5,6},{6,7},{7,4},{8,9},{9,10},{10,1... | collective-permute-start | bytes 36872 | tf_op jit(solution)/shard_map/ppermute | solution.py:625
  32.9 2.4 %collective-permute-start.7 = (f32[24,128]{1,0:T(8,128)S(1)}, f32[24,128]{1,0:T(8,128)S(1)}, u32[]{:S(2)}, u32[]{:S(2)}) collective-permute-start(f32[24,128]{1,0:T(8,128)S(1)} %get-tuple-element.106), channel_id=1, source_target_pairs={{1,0},{2,1},{3,2},{0,3},{5,4},{6,5},{7,6},{4,7},{9,8},{10,9},{11,1... | collective-permute-start | bytes 36872 | tf_op jit(solution)/shard_map/ppermute | solution.py:626
  37.5 3.2 %collective-permute-start.8 = (f32[24,128]{1,0:T(8,128)S(1)}, f32[24,128]{1,0:T(8,128)S(1)}, u32[]{:S(2)}, u32[]{:S(2)}) collective-permute-start(f32[24,128]{1,0:T(8,128)S(1)} %get-tuple-element.110), channel_id=1, source_target_pairs={{0,1},{1,2},{2,3},{3,0},{4,5},{5,6},{6,7},{7,4},{8,9},{9,10},{10,1... | collective-permute-start | bytes 36872 | tf_op jit(solution)/shard_map/ppermute | solution.py:625
  38.3 2.4 %collective-permute-start.9 = (f32[24,128]{1,0:T(8,128)S(1)}, f32[24,128]{1,0:T(8,128)S(1)}, u32[]{:S(2)}, u32[]{:S(2)}) collective-permute-start(f32[24,128]{1,0:T(8,128)S(1)} %get-tuple-element.111), channel_id=1, source_target_pairs={{1,0},{2,1},{3,2},{0,3},{5,4},{6,5},{7,6},{4,7},{9,8},{10,9},{11,1... | collective-permute-start | bytes 36872 | tf_op jit(solution)/shard_map/ppermute | solution.py:626
  40.8 1.8 %copy-start = (bf16[1,120,1024]{2,1,0:T(8,128)(2,1)S(1)}, bf16[1,120,1024]{2,1,0:T(8,128)(2,1)}, u32[]{:S(2)}) copy-start(bf16[1,120,1024]{2,1,0:T(8,128)(2,1)} %refs_8_.1) | copy-start | bytes 737284
  40.8 1.9 %copy-start.8 = (s32[1024]{0:T(1024)S(1)}, s32[1024]{0:T(1024)}, u32[]{:S(2)}) copy-start(s32[1024]{0:T(1024)} %param.27) | copy-start | bytes 12292
  44.4 2.0 %collective-permute-start.10 = (f32[16,17,2,128]{3,2,1,0:T(2,128)S(1)}, f32[16,17,2,128]{3,2,1,0:T(2,128)S(1)}, u32[]{:S(2)}, u32[]{:S(2)}) collective-permute-start(f32[16,17,2,128]{3,2,1,0:T(2,128)S(1)} %get-tuple-element.128), channel_id=1, source_target_pairs={{0,1},{1,0},{2,3},{3,2},{4,5},{5,4},{6,7},{7,6},{8,9},{9,8},{10,11... | collective-permute-start | bytes 835592 | tf_op jit(solution)/shard_map/ppermute | solution.py:640
